TPU v7x, 256 devices: a whole 4x4x8 slice. The times are simulated.
256 devices in a mesh: dp: 8 (over y, core), seq: 32 (over x, z).
Axes of the slice: x: 4, y: 4, z: 8, core: 2. Of those that a mesh axis runs over, the one named last changes fastest.
Arguments:
- tokens: bfloat16 [262144, 2048], P(('dp', 'seq')), parts along dimension 0, may hold values from -6 to 6
- chosen: int32 [32768], P('dp'), parts along dimension 0, may hold values from 0 to 32767, as said below
- gates: float32 [32768], P('dp'), parts along dimension 0, may hold values from 0.5 to 2
- w_query: bfloat16 [2048, 1024], P('seq'), may hold values from -1.8561553 to 1.8561553
- w_key: bfloat16 [2048, 256], P('seq'), may hold values from -0.088388348 to 0.088388348
- w_value: bfloat16 [2048, 256], P('seq'), may hold values from -0.125 to 0.125
- w_out: bfloat16 [1024, 2048], P(None, 'seq'), may hold values from -0.5 to 0.5
Outputs:
- mixed: bfloat16 [262144, 2048], P(('dp', 'seq')), parts along dimension 0
There are 8 independent parts, one for each index of `dp`. A program takes and returns all parts, laid end to end along the dimension named above; an argument that names none is the same for every part. Nothing has to cross between parts.
Inputs may be any that keep to these rules, and one draw needn't show every extreme that they name: `chosen`: distinct positions in increasing order; at most 256 of them lie in one device's 1024 consecutive positions, and exactly 256 lie in some device's positions.
All inputs are finite; a program needn't handle non-finite values.
Results may differ from a plain program's by a relative error of at most 0.006.
Values may be sent and summed in bfloat16 or wider, within the bound.
A program may use at most 128 MiB of HBM per device.

v0:
```python
import math

import jax
import jax.numpy as jnp
from jax import lax
from jax.sharding import PartitionSpec as P

HEADS = 8
KV_HEADS = 2
HEAD_DIM = 128
ROWS_DEV = 128
MOST_OWN = 256


neg_fill = -1e30


def side_by_side(arrays, axis, dim, along):
    widths = [a.shape[along] for a in arrays]
    both = jnp.concatenate(arrays, axis=along)
    result = lax.all_gather(both, axis, axis=dim, tiled=True)
    return tuple(jnp.split(result, [sum(widths[:k]) for k in range(1, len(widths))], axis=along))


def normalize(row_block):
    widened = row_block.astype(jnp.float32)
    scale_rows = lax.rsqrt(jnp.mean(widened * widened, axis=1, keepdims=True) + 1e-06)
    return (widened * scale_rows).astype(jnp.bfloat16)


def per_device(tokens, chosen, gates, w_query, w_key, w_value, w_out):
    shards = lax.axis_size("seq")
    my_index = lax.axis_index("seq")
    tok_rows = tokens.shape[0]
    model_width = tokens.shape[1]
    picked_total = chosen.shape[0]
    slot_count = (MOST_OWN - 1) // shards + 1
    group_size = HEADS // KV_HEADS
    owner_of = chosen // tok_rows
    owners = jnp.arange(shards, dtype=jnp.int32)
    counts = jnp.sum((owner_of[None, :] == owners[:, None]).astype(jnp.int32), axis=1)
    starts = jnp.cumsum(counts) - counts
    my_start = starts[my_index]
    my_count = counts[my_index]
    my_base = my_index * tok_rows
    own_steps = jnp.arange(MOST_OWN, dtype=jnp.int32)
    own_valid = own_steps < my_count
    slot_steps = jnp.arange(slot_count, dtype=jnp.int32)
    lead_step = (owners - my_start) % shards
    offset = lead_step[:, None] + shards * slot_steps[None, :]
    is_valid = offset < my_count
    flat_ids = jnp.clip((my_start + offset).reshape(-1), 0, picked_total - 1)
    flat_valid = is_valid.reshape(-1)
    spot_row = jnp.where(flat_valid, chosen[flat_ids] - my_base, 0)
    row_block = normalize(tokens[spot_row])
    outgoing = jnp.where(flat_valid[:, None], row_block, jnp.zeros_like(row_block)).reshape(
        shards, slot_count, model_width
    )
    arrived = lax.all_to_all(outgoing, "seq", split_axis=0, concat_axis=0, tiled=True)
    local_rows = jnp.arange(ROWS_DEV, dtype=jnp.int32)
    query_order = my_index + shards * local_rows
    source = owner_of[query_order]
    place_at = source * slot_count + (query_order - starts[source]) // shards
    normed = arrived.reshape(shards * slot_count, model_width)[place_at]

    def key_order_of(row_ids):
        return row_ids // ROWS_DEV + shards * (row_ids % ROWS_DEV)

    rows_here = normed.shape[0]
    pieces = side_by_side((w_query, w_key, w_value), "seq", 0, 1)
    query_sum, key_sum, value_sum = tuple(
        (jnp.dot(normed, piece_now, preferred_element_type=jnp.float32) for piece_now in pieces)
    )
    query_matrix = (
        (query_sum * HEAD_DIM ** (-0.5))
        .astype(jnp.bfloat16)
        .reshape(rows_here, KV_HEADS, group_size, HEAD_DIM)
    )
    keys_all = key_sum.astype(jnp.bfloat16)
    values = value_sum.astype(jnp.bfloat16)
    start_state = (
        jnp.full((KV_HEADS, group_size, rows_here), neg_fill, jnp.float32),
        jnp.zeros((KV_HEADS, group_size, rows_here), jnp.float32),
        jnp.zeros((KV_HEADS, group_size, rows_here, HEAD_DIM), jnp.float32),
    )
    key_rows, value_rows = side_by_side((keys_all, values), "seq", 0, 1)
    length = key_rows.shape[0]
    block_rows = math.gcd(length, 512)

    def one_block(step_no, inner_state):
        top_score, weight, mixed_sum = inner_state
        first_row = step_no * block_rows
        key_portion = lax.dynamic_slice_in_dim(key_rows, first_row, block_rows, 0).reshape(
            block_rows, KV_HEADS, HEAD_DIM
        )
        value_piece = lax.dynamic_slice_in_dim(value_rows, first_row, block_rows, 0).reshape(
            block_rows, KV_HEADS, HEAD_DIM
        )
        key_order = key_order_of(first_row + jnp.arange(block_rows, dtype=jnp.int32))
        logit_scores = jnp.einsum(
            "qjfh,ujh->jfqu", query_matrix, key_portion, preferred_element_type=jnp.float32
        )
        allowed = key_order[None, :] <= query_order[:, None]
        logit_scores = jnp.where(allowed, logit_scores, neg_fill)
        fresh_top = jnp.maximum(top_score, jnp.max(logit_scores, axis=-1))
        weights_now = jnp.where(allowed, jnp.exp(logit_scores - fresh_top[..., None]), 0.0)
        shrink = jnp.exp(top_score - fresh_top)
        weight = weight * shrink + jnp.sum(weights_now, axis=-1)
        mixed_sum = mixed_sum * shrink[..., None] + jnp.einsum(
            "yoih,hyf->yoif",
            weights_now.astype(jnp.bfloat16),
            value_piece,
            preferred_element_type=jnp.float32,
        )
        return (fresh_top, weight, mixed_sum)

    top_score, weight, mixed_sum = lax.fori_loop(0, length // block_rows, one_block, start_state)
    attended = (
        jnp.transpose(mixed_sum / weight[..., None], (2, 0, 1, 3))
        .reshape(rows_here, HEADS * HEAD_DIM)
        .astype(jnp.bfloat16)
    )
    block_out = jnp.dot(
        attended,
        lax.all_gather(w_out, "seq", axis=1, tiled=True),
        preferred_element_type=jnp.float32,
    ).astype(jnp.bfloat16)
    own_compact = jnp.clip(my_start + own_steps, 0, picked_total - 1)
    slot_steps = jnp.arange(slot_count, dtype=jnp.int32)
    lead_back = (my_index - starts) % shards
    offset_back = lead_back[:, None] + shards * slot_steps[None, :]
    valid_back = offset_back < counts[:, None]
    local_k = jnp.clip((starts[:, None] + offset_back - my_index) // shards, 0, ROWS_DEV - 1)
    outgoing_back = jnp.where(
        valid_back[..., None], block_out[local_k], jnp.zeros((), jnp.bfloat16)
    )
    returned = lax.all_to_all(outgoing_back, "seq", split_axis=0, concat_axis=0, tiled=True)
    pick_at = (my_start + own_steps) % shards * slot_count + jnp.clip(
        own_steps // shards, 0, slot_count - 1
    )
    delta_rows = returned.reshape(shards * slot_count, model_width)[pick_at]
    spot_row = jnp.where(own_valid, chosen[own_compact] - my_base, tok_rows)
    lift_rows = gates[own_compact][:, None] * delta_rows.astype(jnp.float32)
    mixed = tokens.astype(jnp.float32).at[spot_row].add(lift_rows, mode="drop")
    return mixed.astype(jnp.bfloat16)


def solution(mesh):
    return jax.shard_map(
        per_device,
        mesh=mesh,
        in_specs=(
            P(("dp", "seq"), None),
            P("dp"),
            P("dp"),
            P("seq", None),
            P("seq", None),
            P("seq", None),
            P(None, "seq"),
        ),
        out_specs=P(("dp", "seq"), None),
        check_vma=False,
    )
```

profile of v0, /device:TPU:8, one launch (start us, length us, event | category | flops | bytes accessed | tf_op | source)
XLA Modules:
  0.0 335.7 jit_solution(2853415803978076880)
XLA Ops:
  6.5 1.7 pad_maximum_fusion
  13.1 2.0 gather_fusion.2
  15.1 5.1 %gather_fusion.3 = bf16[256,2048]{1,0:T(8,128)(2,1)S(1)} fusion(bf16[1024,2048]{1,0:T(8,128)(2,1)} %param.9, s32[1024]{0:T(1024)S(1)} %pad_clamp_fusion.5), kind=kCustom, calls=%fused_computation.3 | custom fusion | bytes 2098176 | tf_op jit(solution)/shard_map/gather | solution.py:55
  20.6 1.3 fusion.31
  21.9 11.3 %all-to-all-start = ((bf16[32,8,2048]{2,1,0:T(8,128)(2,1)}), bf16[32,8,2048]{2,1,0:T(8,128)(2,1)S(1)}, u32[]{:S(2)}, u32[]{:S(2)}) async-start(bf16[32,8,2048]{2,1,0:T(8,128)(2,1)} %fusion.31), calls=%async_computation | async-start | bytes 2097152 | tf_op jit(solution)/shard_map/all_to_all | solution.py:59
  33.3 1.1 gather_fusion.4
  34.4 1.2 gather_fusion.5
  35.7 28.9 %all-to-all-done = bf16[32,8,2048]{2,1,0:T(8,128)(2,1)S(1)} async-done(((bf16[32,8,2048]{2,1,0:T(8,128)(2,1)}), bf16[32,8,2048]{2,1,0:T(8,128)(2,1)S(1)}, u32[]{:S(2)}, u32[]{:S(2)}) %all-to-all-start) | async-done | bytes 1048608 | tf_op jit(solution)/shard_map/all_to_all | solution.py:59
  65.5 42.5 %all-gather.4.cloned.1.call-done = bf16[2048,1536]{1,0:T(8,128)(2,1)} async-done(((bf16[64,1536]{1,0:T(8,128)(2,1)}), bf16[2048,1536]{1,0:T(8,128)(2,1)}) %all-gather.4.cloned.1.call-update) | async-done | bytes 6291472 | tf_op jit(solution)/shard_map/all_gather | solution.py:21
  108.0 1.5 convolution_convert_fusion.1
  109.5 1.5 convolution_convert_fusion.2
  112.8 2.9 fusion.28
  116.0 74.6 %all-gather.6.cloned.1.call-done = bf16[4096,512]{1,0:T(8,128)(2,1)} async-done(((bf16[128,512]{1,0:T(8,128)(2,1)}), bf16[4096,512]{1,0:T(8,128)(2,1)}) %all-gather.6.cloned.1.call-update) | async-done | bytes 4194320 | tf_op jit(solution)/shard_map/all_gather | solution.py:21
  190.6 3.8 %fusion.53 = (bf16[4096,256]{1,0:T(8,128)(2,1)S(1)}, bf16[4096,256]{1,0:T(8,128)(2,1)}) fusion(bf16[4096,512]{1,0:T(8,128)(2,1)} %all-gather.6.cloned.1.call-done), kind=kLoop, calls=%fused_computation.143 | loop fusion | bytes 8388608 | tf_op jit(solution)/shard_map/split | solution.py:22
  194.4 33.7 %while.20 = (s32[]{:T(128)}, f32[2,4,128]{2,1,0:T(4,128)S(1)}, f32[2,4,128]{2,1,0:T(4,128)S(1)}, f32[2,4,128,128]{3,2,1,0:T(8,128)}, bf16[4096,256]{1,0:T(8,128)...) while((s32[]{:T(128)}, f32[2,4,128]{2,1,0:T(4,128)S(1)}, ...), condition=%wide.region_6.7_spmd.clone, body=%wide.region_3.6_spmd.clone.sunk | while | flops 274153728 | bytes 14750971 | solution.py:117
  203.0 1.0 constant_dynamic-slice_fusion.3
  207.2 1.0 constant_dynamic-slice_fusion.3
  215.6 1.0 constant_dynamic-slice_fusion.3
  219.8 1.0 constant_dynamic-slice_fusion.3
  224.1 1.0 constant_dynamic-slice_fusion.3
  228.1 1.2 copy.38
  229.4 42.3 %all-gather.8.cloned.1.call-done = bf16[1024,2048]{0,1:T(8,128)(2,1)} async-done(((bf16[1024,64]{0,1:T(8,128)(2,1)}), bf16[1024,2048]{0,1:T(8,128)(2,1)}) %all-gather.8.cloned.1.call-update) | async-done | bytes 4194320 | tf_op jit(solution)/shard_map/all_gather | solution.py:125
  271.7 3.7 %convolution_convert_fusion = bf16[128,2048]{1,0:T(8,128)(2,1)S(1)} fusion(bf16[128,1024]{0,1:T(8,128)(2,1)S(1)} %bitcast.93, bf16[1024,2048]{0,1:T(8,128)(2,1)} %all-gather.8.cloned.1.call-done), kind=kOutput, calls=%fused_computation.47 | convolution fusion | flops 537133056 | bytes 4980736 | tf_op jit(solution)/shard_map/dot_general | solution.py:123
  275.4 1.4 gather_fusion.7
  276.8 1.1 bitcast_select_fusion.1
  277.9 5.6 %all-to-all-start.1 = ((bf16[32,8,2048]{2,1,0:T(8,128)(2,1)}), bf16[32,8,2048]{2,1,0:T(8,128)(2,1)S(1)}, u32[]{:S(2)}, u32[]{:S(2)}) async-start(bf16[32,8,2048]{2,1,0:T(8,128)(2,1)} %bitcast_select_fusion.1), calls=%async_computation.1 | async-start | bytes 2097152 | tf_op jit(solution)/shard_map/all_to_all | solution.py:137
  283.5 6.5 %convert_element_type.56 = f32[1024,2048]{1,0:T(8,128)} convert(bf16[1024,2048]{1,0:T(8,128)(2,1)} %param.9) | non-fusion elementwise | flops 2097152 | bytes 12582912 | tf_op jit(solution)/shard_map/convert_element_type | solution.py:144
  290.6 1.7 gather_fusion
  292.4 1.7 gather_fusion.1
  294.8 14.5 %all-to-all-done.1 = bf16[32,8,2048]{2,1,0:T(8,128)(2,1)S(1)} async-done(((bf16[32,8,2048]{2,1,0:T(8,128)(2,1)}), bf16[32,8,2048]{2,1,0:T(8,128)(2,1)S(1)}, u32[]{:S(2)}, u32[]{:S(2)}) %all-to-all-start.1) | async-done | bytes 1048608 | tf_op jit(solution)/shard_map/all_to_all | solution.py:137
  309.3 13.7 %scatter_custom_fusion = f32[1024,2048]{1,0:T(8,128)} fusion(f32[1024,2048]{1,0:T(8,128)} %convert_element_type.56, s32[256]{0:T(256)S(1)} %bitcast.101, f32[256]{0:T(256)S(1)} %gather_fusion.1, bf16[256,2048]{1,0:T(8,128)(2,1)S(1)} %bitcast.92, s32[1024]{0:T(1024)S(1)} %pad_clamp_fusion), kind=kCustom, calls=%fused_computation.51 | custom fusion | flops 1572864 | bytes 9442304 | tf_op jit(solution)/shard_map/scatter-add | solution.py:144
  323.1 6.0 %convert_element_type.70 = bf16[1024,2048]{1,0:T(8,128)(2,1)} convert(f32[1024,2048]{1,0:T(8,128)} %scatter_custom_fusion) | non-fusion elementwise | flops 2097152 | bytes 12582912 | tf_op jit(solution)/shard_map/convert_element_type | solution.py:145
  (180 shorter events, 37.8 us)
Async XLA Ops:
  6.5 285.8 %copy-start = (f32[4096]{0:T(1024)S(1)}, f32[4096]{0:T(1024)}, u32[]{:S(2)}) copy-start(f32[4096]{0:T(1024)} %param.11) | copy-start | bytes 49156
  6.5 101.5 %all-gather.4.cloned.1.call-start = ((), (), s32[]{:S(2)}) async-start(), calls=%async_computation.2 | async-start | bytes 6488064 | tf_op jit(solution)/shard_map/all_gather | solution.py:21
  21.9 42.7 %all-to-all-start = ((bf16[32,8,2048]{2,1,0:T(8,128)(2,1)}), bf16[32,8,2048]{2,1,0:T(8,128)(2,1)S(1)}, u32[]{:S(2)}, u32[]{:S(2)}) async-start(bf16[32,8,2048]{2,1,0:T(8,128)(2,1)} %fusion.31), calls=%async_computation | async-start | bytes 2097152 | tf_op jit(solution)/shard_map/all_to_all | solution.py:59
  33.2 157.4 %all-gather.6.cloned.1.call-start = ((), (), s32[]{:S(2)}) async-start(), calls=%async_computation.3 | async-start | bytes 4325376 | tf_op jit(solution)/shard_map/all_gather | solution.py:21
  111.8 159.9 %all-gather.8.cloned.1.call-start = ((), (), s32[]{:S(2)}) async-start(), calls=%async_computation.4 | async-start | bytes 4325376 | tf_op jit(solution)/shard_map/all_gather | solution.py:125
  195.8 1.0 copy-start.2
  197.8 0.8 copy-start.3
  200.0 1.0 copy-start.2
  202.0 0.8 copy-start.3
  204.3 1.0 copy-start.2
  206.2 0.8 copy-start.3
  208.5 1.0 copy-start.2
  210.4 0.8 copy-start.3
  212.7 1.1 copy-start.2
  214.7 0.8 copy-start.3
  216.9 1.0 copy-start.2
  218.9 0.8 copy-start.3
  221.1 1.0 copy-start.2
  223.1 0.8 copy-start.3
  225.4 1.0 copy-start.2
  227.3 0.8 copy-start.3
  277.9 31.4 %all-to-all-start.1 = ((bf16[32,8,2048]{2,1,0:T(8,128)(2,1)}), bf16[32,8,2048]{2,1,0:T(8,128)(2,1)S(1)}, u32[]{:S(2)}, u32[]{:S(2)}) async-start(bf16[32,8,2048]{2,1,0:T(8,128)(2,1)} %bitcast_select_fusion.1), calls=%async_computation.1 | async-start | bytes 2097152 | tf_op jit(solution)/shard_map/all_to_all | solution.py:137
  283.5 7.1 %copy-start.1 = (s32[4096]{0:T(1024)S(1)}, s32[4096]{0:T(1024)}, u32[]{:S(2)}) copy-start(s32[4096]{0:T(1024)} %param.10) | copy-start | bytes 49156
Sparse Core Ops, SparseCore 0:
  9.9 98.0 all-gather.3
  111.9 78.6 all-gather.5
  193.2 78.5 all-gather.7
where the time goes:
time: 337 us; the launch traced here: 336 us
  waiting for transfers between devices  203 us (60%)
  other arithmetic  41 us (12%)
  local copies, waits for them, and re-layouts  39.4 us (12%)
  matrix products  20.9 us (6%)
  starting transfers between devices  17.2 us (5%)
  between operations  13.4 us (4%)
    all_gather x2, waiting for transfers between devices, side_by_side(): result = lax.all_gather(both, axis, axis=dim, tiled=True)  117 us
    all_gather x1, waiting for transfers between devices, per_device(): lax.all_gather(w_out, 'seq', axis=1, tiled=True)  42.3 us
    all_to_all x1, waiting for transfers between devices, per_device(): lax.all_to_all(outgoing, 'seq', split_axis=0, concat_axis=0, tiled=True)  28.9 us
    all_to_all x1, waiting for transfers between devices, per_device(): lax.all_to_all(outgoing_back, 'seq', split_axis=0, concat_axis=0, tiled=T...  14.5 us
    scatter-add x1, other arithmetic, per_device(): mixed = tokens.astype(jnp.float32).at[spot_row].add(lift_rows, mode='drop')  13.7 us
    all_to_all x1, starting transfers between devices, per_device(): lax.all_to_all(outgoing, 'seq', split_axis=0, concat_axis=0, tiled=True)  11.3 us
    dynamic_slice x16, local copies, waits for them, and re-layouts, one_block(): lax.dynamic_slice_in_dim(value_rows, first_row, block_rows, 0)  9.08 us
    dot_general x8, matrix products, one_block(): jnp.einsum('yoih,hyf->yoif', weights_now.astype(jnp.bfloat16), value_piec...  7.21 us
  transfers between devices with their start and end apart: 5, of which 5 were waited for; matrix products, arithmetic and copies ran while one was open for 19% of the time, Pallas kernels for 0%

commit v1 on v0

v1 whole, which is shorter than its diff:
```python
import functools

import jax
import jax.numpy as jnp
from jax import lax
from jax.experimental import pallas as pl
from jax.experimental.pallas import tpu as pltpu
from jax.sharding import PartitionSpec as P

HEADS = 8
KV_HEADS = 2
GROUP = HEADS // KV_HEADS
HEAD_DIM = 128
D = 2048
QW = HEADS * HEAD_DIM
KW = KV_HEADS * HEAD_DIM
W = QW + 2 * KW
SEQ = 32
NX = 4
NZ = 8
TOK = 1024
CHOSEN = 4096
ROWS = 128
MOST = 256
SLOTS = 8
DEPTH = D // SEQ
HALF = DEPTH // 2
MESH = pl.DeviceIdType.MESH
F32 = jnp.float32
BF16 = jnp.bfloat16
FAR = -1e30


def ring_steps(a, b, na, nb, index_of, start, wait, arrived):
    def node(da, db):
        return index_of(lax.rem(a + da + na, na), lax.rem(b + db + nb, nb))

    def reach(order, n):
        return (n // 2, n // 2 - 1) if order % 2 == 0 else (n // 2 - 1, n // 2)

    def first():
        own = node(0, 0)
        for da, db in ((1, 0), (-1, 0), (0, 1), (0, -1)):
            start(own, node(da, db))

    def along_a(k, side):
        block = node(-side * k, 0)
        wait(block)
        limit = na // 2 if side == 1 else na // 2 - 1
        if k < limit:
            start(block, node(side, 0))
        start(block, node(0, 1))
        start(block, node(0, -1))
        arrived(block)

    def along_b(order, j, m, side):
        block = node(j, -side * m)
        wait(block)
        limit = reach(order, nb)[0 if side == 1 else 1]
        if m < limit:
            start(block, node(0, side))
        arrived(block)

    steps = [first]
    columns = [0]
    for k in range(1, na // 2 + 1):
        steps.append(functools.partial(along_a, k, 1))
        columns.append(-k)
        if k < na // 2:
            steps.append(functools.partial(along_a, k, -1))
            columns.append(k)
    for m in range(1, nb // 2 + 1):
        for order, j in enumerate(columns):
            plus, minus = reach(order, nb)
            if m <= plus:
                steps.append(functools.partial(along_b, order, j, m, 1))
            if m <= minus:
                steps.append(functools.partial(along_b, order, j, m, -1))
    return steps


def block_kernel(
    tokens, wq, wk, wv, wo, crow, grow, c2, c2t,
    out, meta,
    tok, weights, wots, wo_in, normed, onehot, bias, query, att, kv_slots, kv_in, kv,
    cpos, bar_unused, load_sem, tok_sem, ici_send, w_recv, o_recv, kv_recv, a_send, a_recv,
    d2d_send, d2d_recv,
):
    dp = lax.axis_index("dp")
    me = lax.axis_index("seq")
    core = lax.rem(dp, 2)
    partner = dp + 1 - 2 * core
    x, z = me // NZ, lax.rem(me, NZ)

    w_rows = pl.ds(pl.multiple_of(me * DEPTH, DEPTH), DEPTH)
    loads = [
        pltpu.make_async_copy(wq, weights.at[w_rows, 0:QW], load_sem.at[0]),
        pltpu.make_async_copy(wk, weights.at[w_rows, QW : QW + KW], load_sem.at[1]),
        pltpu.make_async_copy(wv, weights.at[w_rows, QW + KW : W], load_sem.at[2]),
        pltpu.make_async_copy(wo, wo_in, load_sem.at[3]),
    ]
    for copy in loads:
        copy.start()
    token_load = pltpu.make_async_copy(tokens, tok, tok_sem)
    token_load.start()

    barrier = pltpu.get_barrier_semaphore()

    def greet(j, carry):
        pl.semaphore_signal(
            barrier, inc=1, device_id=(dp, lax.rem(me + j, SEQ)), device_id_type=MESH
        )
        return carry

    lax.fori_loop(1, SEQ, greet, 0)
    pl.semaphore_signal(barrier, inc=1, device_id=(partner, me), device_id_type=MESH)
    pl.semaphore_wait(barrier, SEQ)

    def gather(view, recv, stage, shared):
        def ici(block, dest):
            return pltpu.make_async_remote_copy(
                src_ref=view(block, core),
                dst_ref=view(block, core),
                send_sem=ici_send.at[stage],
                recv_sem=recv.at[block],
                device_id=(dp, dest),
                device_id_type=MESH,
            )

        def start(block, dest):
            ici(block, dest).start()

        def wait(block):
            ici(block, lax.rem(me + 1, SEQ)).wait_recv()

        def arrived(block):
            if shared is not None:
                pltpu.make_async_remote_copy(
                    src_ref=view(block, core),
                    dst_ref=view(block, core),
                    send_sem=d2d_send.at[shared],
                    recv_sem=d2d_recv.at[shared],
                    device_id=(partner, me),
                    device_id_type=MESH,
                ).start()

        zfirst = ring_steps(z, x, NZ, NX, lambda p, q: q * NZ + p, start, wait, arrived)
        xfirst = ring_steps(x, z, NX, NZ, lambda p, q: p * NZ + q, start, wait, arrived)

        def run(low, high):
            @pl.when(core == 0)
            def _():
                for step in zfirst[low:high]:
                    step()

            @pl.when(core == 1)
            def _():
                for step in xfirst[low:high]:
                    step()

        return run, len(zfirst)

    def drain(whole, stage, shared):
        pltpu.make_async_copy(whole, whole, ici_send.at[stage]).wait()
        if shared is not None:
            pltpu.make_async_copy(whole, whole, d2d_send.at[shared]).wait()
            pltpu.make_async_copy(whole, whole, d2d_recv.at[shared]).wait()

    def half_rows(block, half):
        start = block * DEPTH + half * HALF
        return pl.ds(pl.multiple_of(start, HALF), HALF)

    w_run, w_steps = gather(lambda s, c: weights.at[half_rows(s, c), :], w_recv, 0, 0)
    o_run, o_steps = gather(lambda s, c: wots.at[half_rows(s, c), :], o_recv, 1, 1)
    kv_run, kv_steps = gather(
        lambda s, c: kv.at[pl.ds(pl.multiple_of(s * ROWS, ROWS), ROWS), :], kv_recv, 2, None
    )

    for copy in loads[:3]:
        copy.wait()
    w_run(0, 1)

    base = (me * TOK).astype(F32)
    listed = crow[...]
    first = jnp.sum(jnp.where(listed < base, 1.0, 0.0), axis=1, keepdims=True)
    last = jnp.sum(jnp.where(listed < base + TOK, 1.0, 0.0), axis=1, keepdims=True)
    shift = jnp.minimum(first, float(CHOSEN - MOST))

    def pick(i, carry):
        rows = pl.ds(pl.multiple_of(i * 32, 32), 32)
        lane = lax.broadcasted_iota(jnp.int32, (32, CHOSEN), 1).astype(F32)
        rank = lax.broadcasted_iota(jnp.int32, (32, 1), 0).astype(F32)
        hit = lane == rank + (shift + (i * 32).astype(F32))
        spot = jnp.sum(jnp.where(hit, crow[...], 0.0), axis=1, keepdims=True)
        gate = jnp.sum(jnp.where(hit, grow[...], 0.0), axis=1, keepdims=True)
        cpos[0, rows, :] = jnp.broadcast_to(spot, (32, 128))
        cpos[1, rows, :] = jnp.broadcast_to(gate, (32, 128))
        return carry

    lax.fori_loop(0, MOST // 32, pick, 0)
    spot = cpos[0, :, 0:1]
    gate = cpos[1, :, 0:1]
    eye = lax.broadcasted_iota(jnp.int32, (MOST, MOST), 0) == lax.broadcasted_iota(
        jnp.int32, (MOST, MOST), 1
    )
    meta[0:1, :] = jnp.sum(jnp.where(eye, spot - base, 0.0), axis=0, keepdims=True)
    meta[1:2, :] = jnp.sum(jnp.where(eye, gate, 0.0), axis=0, keepdims=True)
    place = lax.broadcasted_iota(jnp.int32, (MOST, TOK), 1).astype(F32)
    onehot[...] = jnp.where(place == spot - base, 1.0, 0.0).astype(BF16)

    token_load.wait()
    loads[3].wait()
    unit = jnp.where(
        lax.broadcasted_iota(jnp.int32, (DEPTH, DEPTH), 0)
        == lax.broadcasted_iota(jnp.int32, (DEPTH, DEPTH), 1),
        1.0,
        0.0,
    ).astype(BF16)
    wots[w_rows, :] = lax.dot_general(
        unit, wo_in[...], (((1,), (1,)), ((), ())), preferred_element_type=F32
    ).astype(BF16)

    def gather_rows(n, square):
        columns = pl.ds(pl.multiple_of(n * 256, 256), 256)
        part = jnp.dot(onehot[...], tok[:, columns], preferred_element_type=F32)
        normed[:, columns] = part.astype(BF16)
        return square + jnp.sum(part * part, axis=1, keepdims=True)

    square = lax.fori_loop(0, D // 256, gather_rows, jnp.zeros((MOST, 1), F32))
    scale = lax.rsqrt(square * (1.0 / D) + 1e-06)

    def normalize(n, carry):
        columns = pl.ds(pl.multiple_of(n * 256, 256), 256)
        normed[:, columns] = (normed[:, columns].astype(F32) * scale).astype(BF16)
        return carry

    lax.fori_loop(0, D // 256, normalize, 0)

    w_run(1, w_steps)
    drain(weights.at[pl.ds(0, HALF * (SEQ - 1)), :], 0, 0)

    def project_kv(n, carry):
        columns = pl.ds(pl.multiple_of(QW + n * 256, 256), 256)
        part = jnp.dot(normed[...], weights[:, columns], preferred_element_type=F32)
        query[:, pl.ds(pl.multiple_of(n * 256, 256), 256)] = part.astype(BF16)
        return carry

    lax.fori_loop(0, 2, project_kv, 0)

    order = lax.broadcasted_iota(jnp.int32, (MOST, MOST), 1)
    slot = lax.broadcasted_iota(jnp.int32, (MOST, MOST), 0)
    rank = order + shift.astype(jnp.int32)
    offset = rank - first.astype(jnp.int32)
    inside = jnp.where(offset >= 0, 1, 0) * jnp.where(rank < last.astype(jnp.int32), 1, 0)
    goes = (rank & (SEQ - 1)) * SLOTS + (offset >> 5)
    deal = jnp.where(goes == slot, inside, 0).astype(F32).astype(BF16)
    leaving = jnp.dot(deal, query[:, 0 : 2 * KW], preferred_element_type=F32)
    kv_slots[...] = leaving.reshape(SEQ, SLOTS, 2 * KW).astype(BF16)

    def slot_copy(j):
        dest = lax.rem(me + j, SEQ)
        return pltpu.make_async_remote_copy(
            src_ref=kv_slots.at[dest],
            dst_ref=kv_in.at[me],
            send_sem=a_send,
            recv_sem=a_recv,
            device_id=(dp, dest),
            device_id_type=MESH,
        )

    def send_slot(j, carry):
        slot_copy(j).start()
        return carry

    lax.fori_loop(1, SEQ, send_slot, 0)
    kv_in[me] = kv_slots[me]

    def project_q(n, carry):
        columns = pl.ds(pl.multiple_of(n * 256, 256), 256)
        part = jnp.dot(normed[...], weights[:, columns], preferred_element_type=F32)
        query[:, columns] = (part * HEAD_DIM ** (-0.5)).astype(BF16)
        return carry

    lax.fori_loop(0, QW // 256, project_q, 0)

    lane32 = lax.broadcasted_iota(jnp.int32, (ROWS, SEQ), 1)
    mine = jnp.sum(jnp.where(lane32 == me, c2[...], 0.0), axis=1, keepdims=True)
    source = jnp.floor(mine * (1.0 / TOK))

    def before(i, total):
        columns = pl.ds(pl.multiple_of(i * 1024, 1024), 1024)
        return total + jnp.sum(
            jnp.where(crow[:, columns] < source * TOK, 1.0, 0.0), axis=1, keepdims=True
        )

    starts = lax.fori_loop(0, CHOSEN // 1024, before, jnp.zeros((ROWS, 1), F32))
    my_rank = lax.broadcasted_iota(jnp.int32, (ROWS, 1), 0).astype(F32) * SEQ + me.astype(F32)
    found = source * SLOTS + jnp.floor((my_rank - starts) * (1.0 / SEQ))
    take = jnp.where(
        lax.broadcasted_iota(jnp.int32, (ROWS, MOST), 1).astype(F32) == found, 1.0, 0.0
    ).astype(BF16)

    def bias_block(i, carry):
        columns = pl.ds(pl.multiple_of(i * ROWS, ROWS), ROWS)
        bias[:, columns] = jnp.where(c2t[pl.ds(i, 1), :] <= spot, 0.0, FAR)
        return carry

    lax.fori_loop(0, SEQ, bias_block, 0)

    pltpu.make_async_copy(
        kv_in.at[pl.ds(0, SEQ - 1)], kv_in.at[pl.ds(0, SEQ - 1)], a_recv
    ).wait()
    came = kv_in[...].astype(F32).reshape(MOST, 2 * KW).astype(BF16)
    kv[pl.ds(pl.multiple_of(me * ROWS, ROWS), ROWS), :] = jnp.dot(
        take, came, preferred_element_type=F32
    ).astype(BF16)
    kv_run(0, kv_steps)
    o_run(0, 1)

    CHUNK = 1024
    done = 1
    for head in range(HEADS):
        e = head // GROUP
        q = query[:, head * HEAD_DIM : (head + 1) * HEAD_DIM]

        def one_chunk(i, state):
            top, total, acc = state
            rows = pl.ds(pl.multiple_of(i * CHUNK, CHUNK), CHUNK)
            keys = kv[rows, e * HEAD_DIM : (e + 1) * HEAD_DIM]
            values = kv[rows, KW + e * HEAD_DIM : KW + (e + 1) * HEAD_DIM]
            scores = lax.dot_general(
                q, keys, (((1,), (1,)), ((), ())), preferred_element_type=F32
            )
            scores = scores + bias[:, rows]
            fresh = jnp.maximum(top, jnp.max(scores, axis=1, keepdims=True))
            probs = jnp.exp(scores - fresh)
            shrink = jnp.exp(top - fresh)
            total = total * shrink + jnp.sum(probs, axis=1, keepdims=True)
            acc = acc * shrink + jnp.dot(
                probs.astype(BF16), values, preferred_element_type=F32
            )
            return fresh, total, acc

        state = (
            jnp.full((MOST, 1), FAR, F32),
            jnp.zeros((MOST, 1), F32),
            jnp.zeros((MOST, HEAD_DIM), F32),
        )
        top, total, acc = lax.fori_loop(0, CHOSEN // CHUNK, one_chunk, state)
        att[:, head * HEAD_DIM : (head + 1) * HEAD_DIM] = (acc / total).astype(BF16)
        until = 1 + (o_steps - 1) * (head + 1) // HEADS
        o_run(done, until)
        done = until

    drain(wots.at[pl.ds(0, HALF * (SEQ - 1)), :], 1, 1)
    pltpu.make_async_copy(
        kv.at[pl.ds(0, ROWS * (SEQ - 1)), :], kv.at[pl.ds(0, ROWS * (SEQ - 1)), :], ici_send.at[2]
    ).wait()
    pltpu.make_async_copy(
        kv_in.at[pl.ds(0, SEQ - 1)], kv_in.at[pl.ds(0, SEQ - 1)], a_send
    ).wait()

    def project_out(n, carry):
        columns = pl.ds(pl.multiple_of(n * 256, 256), 256)
        out[:, columns] = lax.dot_general(
            att[...], wots[columns, :], (((1,), (1,)), ((), ())), preferred_element_type=F32
        ).astype(BF16)
        return carry

    lax.fori_loop(0, D // 256, project_out, 0)


def mix_kernel(tile, tokens, block_out, meta, mixed):
    i = pl.program_id(0)
    place = lax.broadcasted_iota(jnp.int32, (tile, MOST), 0) + i * tile
    hit = place.astype(F32) == meta[0:1, :]
    gate = jnp.sum(jnp.where(hit, meta[1:2, :], 0.0), axis=1, keepdims=True)
    chosen_row = jnp.where(hit, 1.0, 0.0).astype(BF16)
    for n in range(D // 256):
        columns = slice(n * 256, (n + 1) * 256)
        rows = jnp.dot(chosen_row, block_out[:, columns], preferred_element_type=F32)
        mixed[:, columns] = (tokens[:, columns].astype(F32) + gate * rows).astype(BF16)


def per_device(tokens, chosen, gates, w_query, w_key, w_value, w_out):
    spots = chosen.astype(F32)
    c2 = spots.reshape(ROWS, SEQ)
    anywhere = pl.BlockSpec(memory_space=pl.ANY)
    inside = pl.BlockSpec(memory_space=pltpu.VMEM)
    dma = pltpu.SemaphoreType.DMA
    block_out, meta = pl.pallas_call(
        block_kernel,
        out_shape=(
            jax.ShapeDtypeStruct((MOST, D), BF16),
            jax.ShapeDtypeStruct((8, MOST), F32),
        ),
        in_specs=[anywhere] * 5 + [inside] * 4,
        out_specs=(inside, inside),
        scratch_shapes=[
            pltpu.VMEM((TOK, D), BF16),
            pltpu.VMEM((D, W), BF16),
            pltpu.VMEM((D, QW), BF16),
            pltpu.VMEM((QW, DEPTH), BF16),
            pltpu.VMEM((MOST, D), BF16),
            pltpu.VMEM((MOST, TOK), BF16),
            pltpu.VMEM((MOST, CHOSEN), F32),
            pltpu.VMEM((MOST, QW), BF16),
            pltpu.VMEM((MOST, QW), BF16),
            pltpu.VMEM((SEQ, SLOTS, 2 * KW), BF16),
            pltpu.VMEM((SEQ, SLOTS, 2 * KW), BF16),
            pltpu.VMEM((CHOSEN, 2 * KW), BF16),
            pltpu.VMEM((2, MOST, 128), F32),
            pltpu.SemaphoreType.REGULAR,
            dma((4,)),
            dma,
            dma((3,)),
            dma((SEQ,)),
            dma((SEQ,)),
            dma((SEQ,)),
            dma,
            dma,
            dma((2,)),
            dma((2,)),
        ],
        compiler_params=pltpu.CompilerParams(
            collective_id=0, has_side_effects=True, vmem_limit_bytes=56 * 1024 * 1024
        ),
        name="block",
    )(
        tokens, w_query, w_key, w_value, w_out,
        spots.reshape(1, CHOSEN), gates.reshape(1, CHOSEN), c2, c2.T,
    )
    tile = 256
    return pl.pallas_call(
        functools.partial(mix_kernel, tile),
        grid=(TOK // tile,),
        out_shape=jax.ShapeDtypeStruct((TOK, D), BF16),
        in_specs=[
            pl.BlockSpec((tile, D), lambda i: (i, 0)),
            pl.BlockSpec((MOST, D), lambda i: (0, 0)),
            pl.BlockSpec((8, MOST), lambda i: (0, 0)),
        ],
        out_specs=pl.BlockSpec((tile, D), lambda i: (i, 0)),
        name="mix",
    )(tokens, block_out, meta)


def solution(mesh):
    return jax.shard_map(
        per_device,
        mesh=mesh,
        in_specs=(
            P(("dp", "seq"), None),
            P("dp"),
            P("dp"),
            P("seq", None),
            P("seq", None),
            P("seq", None),
            P(None, "seq"),
        ),
        out_specs=P(("dp", "seq"), None),
        check_vma=False,
    )
```

time: 337 us -> 130 us (0.39)
  waiting for transfers between devices: 203 us -> 0 us
  Pallas kernels: 0 us -> 125 us
  other arithmetic: 41 us -> 0.72 us
  local copies, waits for them, and re-layouts: 39.4 us -> 2.5 us
  matrix products: 20.9 us -> 0 us
  starting transfers between devices: 17.2 us -> 0 us
  between operations: 13.4 us -> 0.01 us
    all_gather x3 -> x0, waiting for transfers between devices: 159 us -> none  [the longest x2 117 us: side_by_side(): result = lax.all_gather(both, axis, axis=dim, tiled=True)]
    pallas_call x0 -> x2, Pallas kernels: none -> 125 us  [the longest x1 119 us: per_device(): pl.pallas_call(block_kernel, out_shape=(jax.ShapeDtypeStruct((MOST, D), B...]
    all_to_all x2 -> x0, waiting for transfers between devices: 43.4 us -> none  [the longest x1 28.9 us: per_device(): lax.all_to_all(outgoing, 'seq', split_axis=0, concat_axis=0, tiled=True)]
    dot_general x20 -> x0, matrix products: 20.9 us -> none  [the longest x8 7.21 us: one_block(): jnp.einsum('yoih,hyf->yoif', weights_now.astype(jnp.bfloat16), value_piec...]
    all_to_all x2 -> x0, starting transfers between devices: 16.9 us -> none  [the longest x1 11.3 us: per_device(): lax.all_to_all(outgoing, 'seq', split_axis=0, concat_axis=0, tiled=True)]
    gather x8 -> x0, local copies, waits for them, and re-layouts: 15.2 us -> none  [the longest x1 5.09 us: per_device(): row_block = normalize(tokens[spot_row])]
    scatter-add x1 -> x0, other arithmetic: 13.7 us -> none  [per_device(): mixed = tokens.astype(jnp.float32).at[spot_row].add(lift_rows, mode='drop')]
    convert_element_type x3 -> x1, other arithmetic: 12.6 us -> 0.72 us  [per_device(): spots = chosen.astype(F32)]
  transfers between devices with their start and end apart: 5 -> 0, of which waited for: 5 -> 0; matrix products, arithmetic and copies ran while one was open for 19% -> 0% of each run, Pallas kernels for 0% -> 0%
where the time goes in v1:
time: 130 us; the launch traced here: 129 us
  Pallas kernels  125 us (96%)
  local copies, waits for them, and re-layouts  2.5 us (2%)
    pallas_call x1, Pallas kernels, per_device(): pl.pallas_call(block_kernel, out_shape=(jax.ShapeDtypeStruct((MOST, D), B...  119 us
    pallas_call x1, Pallas kernels, per_device(): pl.pallas_call(functools.partial(mix_kernel, tile), grid=(TOK // tile,),...  5.93 us

profile of v1, /device:TPU:8, one launch (start us, length us, event | category | flops | bytes accessed | tf_op | source)
XLA Modules:
  0.0 128.7 jit_solution(17709824082272092874)
XLA Ops:
  0.0 0.7 convert_element_type.3
  0.7 0.0 copy-start.1
  0.7 0.1 reshape.11.c2
  0.8 0.0 copy-start
  0.8 0.7 copy.10
  1.5 1.7 %copy.11.wo = bf16[1024,64]{1,0:T(8,128)(2,1)} copy(bf16[1024,64]{0,1:T(8,128)(2,1)} %param.13) | data formatting | bytes 262144 | tf_op args[6]
  3.2 0.0 copy-done.1
  3.2 0.0 copy-done
  3.2 119.5 %block.1 = (bf16[256,2048]{1,0:T(8,128)(2,1)}, f32[8,256]{1,0:T(8,128)}) custom-call(bf16[1024,2048]{1,0:T(8,128)(2,1)} %tokens.3, bf16[64,1024]{1,0:T(8,128)(2,1)} %wq.1, bf16[64,256]{1,0:T(8,128)(2,1)} %wk.1, bf16[64,256]{1,0:T(8,128)(2,1)} %wv.1, bf16[1024,64]{1,0:T(8,128)(2,1)} %copy.11.wo, f32[1,4096]{1,0:T(1,128)} %bitcast.3, f32[1,4096]{1,0:T(1,128)} %bitcast.5, ...), custom_call_target="tpu_custom_call" | custom-call | tf_op jit(solution)/shard_map/block/pallas_call | solution.py:391
  122.7 5.9 %mix.1 = bf16[1024,2048]{1,0:T(8,128)(2,1)} custom-call(bf16[1024,2048]{1,0:T(8,128)(2,1)} %tokens.3, bf16[256,2048]{1,0:T(8,128)(2,1)} %get-tuple-element.7.block_out, f32[8,256]{1,0:T(8,128)} %get-tuple-element.8.meta), custom_call_target="tpu_custom_call" | custom-call | tf_op jit(solution)/shard_map/mix/pallas_call | solution.py:434
Async XLA Ops:
  0.7 2.5 %copy-start.1 = (f32[4096]{0:T(1024)}, f32[4096]{0:T(1024)S(1)}, u32[]{:S(2)}) copy-start(f32[4096]{0:T(1024)S(1)} %convert_element_type.3) | copy-start | bytes 49156
  0.8 2.4 %copy-start = (f32[128,32]{1,0:T(8,128)}, f32[128,32]{1,0:T(8,128)S(1)}, u32[]{:S(2)}) copy-start(f32[128,32]{1,0:T(8,128)S(1)} %reshape.11.c2) | copy-start | bytes 49156

commit v2 on v1

v2 whole, which is shorter than its diff:
```python
import functools

import jax
import jax.numpy as jnp
from jax import lax
from jax.experimental import pallas as pl
from jax.experimental.pallas import tpu as pltpu
from jax.sharding import PartitionSpec as P

HEADS = 8
KV_HEADS = 2
GROUP = HEADS // KV_HEADS
HEAD_DIM = 128
D = 2048
QW = HEADS * HEAD_DIM
KW = KV_HEADS * HEAD_DIM
SEQ = 32
NX = 4
NZ = 8
TOK = 1024
CHOSEN = 4096
ROWS = 128
MOST = 256
SLOTS = 8
DEPTH = D // SEQ
HALF = DEPTH // 2
PARTS = 8
PIECE = DEPTH // PARTS
CHUNK = 1024
PER = CHUNK // ROWS
LAG = 4
MESH = pl.DeviceIdType.MESH
F32 = jnp.float32
BF16 = jnp.bfloat16
FAR = -1e30


def ring_steps(na, nb, send, wait, arrived):
    def reach(order, n):
        return (n // 2, n // 2 - 1) if order % 2 == 0 else (n // 2 - 1, n // 2)

    def first():
        for to in ((1, 0), (-1, 0), (0, 1), (0, -1)):
            send((0, 0), to)

    def along_a(k, side):
        block = (-side * k, 0)
        wait(block)
        if k < reach(0, na)[0 if side == 1 else 1]:
            send(block, (side, 0))
        send(block, (0, 1))
        send(block, (0, -1))
        arrived(block)

    def along_b(order, j, m, side):
        block = (j, -side * m)
        wait(block)
        if m < reach(order, nb)[0 if side == 1 else 1]:
            send(block, (0, side))
        arrived(block)

    steps, blocks, columns = [first], [(0, 0)], [0]
    for k in range(1, na // 2 + 1):
        for side in (1, -1):
            if k <= reach(0, na)[0 if side == 1 else 1]:
                steps.append(functools.partial(along_a, k, side))
                columns.append(-side * k)
                blocks.append((-side * k, 0))
    for m in range(1, nb // 2 + 1):
        for order, j in enumerate(columns):
            for side in (1, -1):
                if m <= reach(order, nb)[0 if side == 1 else 1]:
                    steps.append(functools.partial(along_b, order, j, m, side))
                    blocks.append((j, -side * m))
    return steps, [(p % na, q % nb) for p, q in blocks]


def block_kernel(
    tokens, wq, wk, wv, wo, crow, grow, c2, c2t,
    out, meta,
    tok, kvw, wqo, normed, onehot, deal, take, bias, query, att, kv_own, kv_slots, kv_in, kv,
    cpos, wide, top_ref, total_ref, acc_ref,
    load_sem, tok_sem, w_send, w_recv, o_send, o_recv, d_send, d_recv, a_send, a_recv,
    kv_send, kv_recv, q_send, q_recv, y_send, y_recv, p_send, p_recv,
):
    dp = lax.axis_index("dp")
    me = lax.axis_index("seq")
    core = lax.rem(dp, 2)
    y = dp // 2
    partner = dp + 1 - 2 * core
    x, z = me // NZ, lax.rem(me, NZ)

    def along_y(k):
        return lax.rem(y + k + 4, 4) * 2 + core

    def zf(block):
        return lax.rem(x + block[1] + NX, NX) * NZ + lax.rem(z + block[0] + NZ, NZ)

    def xf(block):
        return lax.rem(x + block[0] + NX, NX) * NZ + lax.rem(z + block[1] + NZ, NZ)

    def remote(src, dst, send_sem, recv_sem, to_dp, to_seq):
        return pltpu.make_async_remote_copy(
            src_ref=src,
            dst_ref=dst,
            send_sem=send_sem,
            recv_sem=recv_sem,
            device_id=(to_dp, to_seq),
            device_id_type=MESH,
        )

    def kv_unit(s, half):
        start = s * DEPTH + half * HALF
        return pl.ds(pl.multiple_of(start, HALF), HALF)

    own = kv_unit(me, core)
    loads = [
        pltpu.make_async_copy(wk.at[pl.ds(core * HALF, HALF), :], kvw.at[own, 0:KW], load_sem.at[0]),
        pltpu.make_async_copy(wv.at[pl.ds(core * HALF, HALF), :], kvw.at[own, KW : 2 * KW], load_sem.at[1]),
        pltpu.make_async_copy(wq.at[dp], wqo.at[0, me, dp], load_sem.at[2]),
        pltpu.make_async_copy(wo.at[dp], wqo.at[1, me, dp], load_sem.at[3]),
    ]
    for copy in loads:
        copy.start()
    token_load = pltpu.make_async_copy(tokens, tok, tok_sem)
    token_load.start()

    barrier = pltpu.get_barrier_semaphore()

    def greet(j, carry):
        pl.semaphore_signal(
            barrier, inc=1, device_id=(dp, lax.rem(me + j, SEQ)), device_id_type=MESH
        )
        return carry

    lax.fori_loop(1, SEQ, greet, 0)
    for other in (partner, along_y(1), along_y(-1)):
        pl.semaphore_signal(barrier, inc=1, device_id=(other, me), device_id_type=MESH)

    base = (me * TOK).astype(F32)
    listed = crow[...]
    first = jnp.sum(jnp.where(listed < base, 1.0, 0.0), axis=1, keepdims=True)
    last = jnp.sum(jnp.where(listed < base + TOK, 1.0, 0.0), axis=1, keepdims=True)
    shift = jnp.minimum(first, float(CHOSEN - MOST))

    def pick(i, carry):
        rows = pl.ds(pl.multiple_of(i * 32, 32), 32)
        lane = lax.broadcasted_iota(jnp.int32, (32, CHOSEN), 1).astype(F32)
        rank = lax.broadcasted_iota(jnp.int32, (32, 1), 0).astype(F32)
        hit = lane == rank + (shift + (i * 32).astype(F32))
        spot = jnp.sum(jnp.where(hit, crow[...], 0.0), axis=1, keepdims=True)
        gate = jnp.sum(jnp.where(hit, grow[...], 0.0), axis=1, keepdims=True)
        cpos[0, rows, :] = jnp.broadcast_to(spot, (32, 128))
        cpos[1, rows, :] = jnp.broadcast_to(gate, (32, 128))
        return carry

    lax.fori_loop(0, MOST // 32, pick, 0)
    place = lax.broadcasted_iota(jnp.int32, (MOST, TOK), 1).astype(F32)
    onehot[...] = jnp.where(place == cpos[0, :, 0:1] - base, 1.0, 0.0).astype(BF16)

    for copy in loads:
        copy.wait()
    pl.semaphore_wait(barrier, SEQ + 2)

    def q_copy(s, k, slot, to):
        piece = wqo.at[0, s, along_y(k)]
        return remote(piece, piece, q_send, q_recv.at[slot, s], along_y(to), me)

    def to_y(s):
        q_copy(s, 0, 0, 1).start()
        q_copy(s, 0, 1, -1).start()

    def from_y(i):
        s = block_at(i)
        q_copy(s, -1, 0, 1).wait_recv()
        if i % 2 == 0:
            q_copy(s, -1, 2, 1).start()
        q_copy(s, 1, 1, -1).wait_recv()
        if i % 2 == 1:
            q_copy(s, 1, 2, -1).start()

    def first_gather(at):
        def send(block, to):
            s, dest = at(block), at(to)
            half = kvw.at[kv_unit(s, core), :]
            remote(half, half, w_send, w_recv.at[s], dp, dest).start()
            part = wqo.at[:, s, dp]
            remote(part, part, o_send, o_recv.at[s], dp, dest).start()

        def wait(block):
            s, other = at(block), lax.rem(me + 1, SEQ)
            half = kvw.at[kv_unit(s, core), :]
            remote(half, half, w_send, w_recv.at[s], dp, other).wait_recv()
            part = wqo.at[:, s, dp]
            remote(part, part, o_send, o_recv.at[s], dp, other).wait_recv()

        def arrived(block):
            s = at(block)
            half = kvw.at[kv_unit(s, core), :]
            remote(half, half, d_send, d_recv, partner, me).start()
            to_y(s)

        return send, wait, arrived

    def by_core(z_steps, x_steps):
        @pl.when(core == 0)
        def _():
            for step in z_steps:
                step()

        @pl.when(core == 1)
        def _():
            for step in x_steps:
                step()

    z_steps, z_blocks = ring_steps(NZ, NX, *first_gather(zf))
    x_steps, x_blocks = ring_steps(NX, NZ, *first_gather(xf))

    def block_at(i):
        return jnp.where(core == 0, zf(z_blocks[i]), xf(x_blocks[i]))

    def gather_rows(n):
        columns = slice(n * 256, (n + 1) * 256)
        part = jnp.dot(onehot[...], tok[:, columns], preferred_element_type=F32)
        normed[:, columns] = part.astype(BF16)
        square = jnp.broadcast_to(jnp.sum(part * part, axis=1, keepdims=True), (MOST, 128))
        wide[...] = square if n == 0 else wide[...] + square

    def normalize(n):
        columns = slice(n * 512, (n + 1) * 512)
        scale = lax.rsqrt(wide[:, 0:1] * (1.0 / D) + 1e-06)
        normed[:, columns] = (normed[:, columns].astype(F32) * scale).astype(BF16)

    def place_rows():
        order = lax.broadcasted_iota(jnp.int32, (MOST, MOST), 1)
        slot = lax.broadcasted_iota(jnp.int32, (MOST, MOST), 0)
        rank = order + shift.astype(jnp.int32)
        offset = rank - first.astype(jnp.int32)
        inside = jnp.where(offset >= 0, 1, 0) * jnp.where(rank < last.astype(jnp.int32), 1, 0)
        goes = (rank & (SEQ - 1)) * SLOTS + (offset >> 5)
        deal[...] = jnp.where(goes == slot, inside, 0).astype(F32).astype(BF16)
        gate = cpos[1, :, 0:1]
        eye = order == slot
        meta[0:1, :] = jnp.sum(jnp.where(eye, cpos[0, :, 0:1] - base, 0.0), axis=0, keepdims=True)
        meta[1:2, :] = jnp.sum(jnp.where(eye, gate, 0.0), axis=0, keepdims=True)

    def find_slots():
        lane32 = lax.broadcasted_iota(jnp.int32, (ROWS, SEQ), 1)
        mine = jnp.sum(jnp.where(lane32 == me, c2[...], 0.0), axis=1, keepdims=True)
        source = jnp.floor(mine * (1.0 / TOK))

        def before(i, total):
            columns = pl.ds(pl.multiple_of(i * 512, 512), 512)
            return total + jnp.sum(
                jnp.where(crow[:, columns] < source * TOK, 1.0, 0.0), axis=1, keepdims=True
            )

        starts = lax.fori_loop(0, CHOSEN // 512, before, jnp.zeros((ROWS, 1), F32))
        my_rank = lax.broadcasted_iota(jnp.int32, (ROWS, 1), 0).astype(F32) * SEQ + me.astype(F32)
        found = source * SLOTS + jnp.floor((my_rank - starts) * (1.0 / SEQ))
        take[...] = jnp.where(
            lax.broadcasted_iota(jnp.int32, (ROWS, MOST), 1).astype(F32) == found, 1.0, 0.0
        ).astype(BF16)

    def bias_blocks(low, high):
        for slot in range(low, high):
            s = block_at(slot)
            bias[:, slot * ROWS : (slot + 1) * ROWS] = jnp.where(
                c2t[pl.ds(s, 1), :] <= cpos[0, :, 0:1], 0.0, FAR
            )

    work = [functools.partial(gather_rows, n) for n in range(D // 256)]
    work += [functools.partial(normalize, n) for n in range(D // 512)]
    work += [place_rows, find_slots]
    work += [functools.partial(bias_blocks, n, n + 4) for n in range(0, SEQ, 4)]

    by_core(z_steps[0:1], x_steps[0:1])
    half = kvw.at[own, :]
    remote(half, half, d_send, d_recv, partner, me).start()
    to_y(me)
    token_load.wait()
    for i in range(1, SEQ):
        if i <= len(work):
            work[i - 1]()
        by_core(z_steps[i : i + 1], x_steps[i : i + 1])
        if i >= LAG:
            from_y(i - LAG)
    for rest in work[SEQ - 1 :]:
        rest()

    def part(a, k, low=0, high=SEQ):
        return wqo.at[a, pl.ds(low, high - low), along_y(k)]

    def along(a, k, slot, to, low=0, high=SEQ):
        return remote(
            part(a, k, low, high), part(a, k, low, high), y_send, y_recv.at[a, slot], along_y(to), me
        )

    def across(a, k):
        remote(part(a, k), part(a, k), p_send, p_recv.at[a], partner, me).start()

    def y_first(a):
        along(a, 0, 0, 1).start()
        along(a, 0, 1, -1).start()
        across(a, 0)

    def y_second(a):
        along(a, -1, 0, 1).wait_recv()
        along(a, -1, 2, 1, 0, SEQ // 2).start()
        across(a, -1)
        along(a, 1, 1, -1).wait_recv()
        along(a, 1, 3, -1, SEQ // 2, SEQ).start()
        across(a, 1)

    def y_third(a):
        along(a, 2, 2, 1, 0, SEQ // 2).wait_recv()
        along(a, 2, 3, -1, SEQ // 2, SEQ).wait_recv()
        across(a, 2)

    def y_last(a):
        whole = wqo.at[a, :, pl.ds(0, 4)]
        pltpu.make_async_copy(whole, whole, p_recv.at[a]).wait()

    whole = kvw.at[pl.ds(0, HALF * SEQ), :]
    pltpu.make_async_copy(whole, whole, d_recv).wait()

    for n in range(2):
        columns = slice(n * 256, (n + 1) * 256)
        kv_own[:, columns] = jnp.dot(
            normed[...], kvw[:, columns], preferred_element_type=F32
        ).astype(BF16)
    leaving = jnp.dot(deal[...], kv_own[...], preferred_element_type=F32)
    kv_slots[...] = leaving.reshape(SEQ, SLOTS, 2 * KW).astype(BF16)

    def send_slot(j, carry):
        dest = lax.rem(me + j, SEQ)
        remote(kv_slots.at[dest], kv_in.at[me], a_send, a_recv, dp, dest).start()
        return carry

    lax.fori_loop(1, SEQ, send_slot, 0)
    kv_in[me] = kv_slots[me]

    for i in range(SEQ - LAG, SEQ):
        from_y(i)

    def last_of_y(s, carry):
        q_copy(s, 2, 2, 1).wait_recv()
        return carry

    lax.fori_loop(0, SEQ, last_of_y, 0)
    for k in range(4):
        across(0, k)
    y_first(1)

    whole = kv_in.at[pl.ds(0, SEQ - 1)]
    pltpu.make_async_copy(whole, whole, a_recv).wait()
    came = kv_in[...].astype(F32).reshape(MOST, 2 * KW).astype(BF16)
    kv[0:ROWS, :] = jnp.dot(take[...], came, preferred_element_type=F32).astype(BF16)

    def second_gather(at, na, nb, blocks):
        def slot(block, seen_from=(0, 0)):
            return blocks.index(((block[0] - seen_from[0]) % na, (block[1] - seen_from[1]) % nb))

        def rows(n):
            return kv.at[pl.ds(n * ROWS, ROWS), :]

        def send(block, to):
            lands = slot(block, to)
            remote(rows(slot(block)), rows(lands), kv_send, kv_recv.at[lands], dp, at(to)).start()

        def wait(block):
            n = slot(block)
            remote(rows(n), rows(n), kv_send, kv_recv.at[n], dp, lax.rem(me + 1, SEQ)).wait_recv()

        return send, wait, lambda block: None

    zk_steps, _ = ring_steps(NZ, NX, *second_gather(zf, NZ, NX, z_blocks))
    xk_steps, _ = ring_steps(NX, NZ, *second_gather(xf, NX, NZ, x_blocks))

    def attend(g, h):
        columns = pl.ds(pl.multiple_of(h * HEAD_DIM, HEAD_DIM), HEAD_DIM)
        e = h // GROUP
        k_columns = pl.ds(pl.multiple_of(e * HEAD_DIM, HEAD_DIM), HEAD_DIM)
        v_columns = pl.ds(pl.multiple_of(KW + e * HEAD_DIM, HEAD_DIM), HEAD_DIM)
        rows = slice(g * CHUNK, (g + 1) * CHUNK)
        scores = lax.dot_general(
            query[:, columns], kv[rows, k_columns], (((1,), (1,)), ((), ())),
            preferred_element_type=F32,
        )
        scores = scores + bias[:, rows]
        fresh = jnp.max(scores, axis=1, keepdims=True)
        if g > 0:
            before = top_ref[h][:, 0:1]
            fresh = jnp.maximum(before, fresh)
        probs = jnp.exp(scores - fresh)
        total = jnp.sum(probs, axis=1, keepdims=True)
        acc = jnp.dot(probs.astype(BF16), kv[rows, v_columns], preferred_element_type=F32)
        if g > 0:
            shrink = jnp.exp(before - fresh)
            total = total_ref[h][:, 0:1] * shrink + total
            acc = acc_ref[h] * shrink + acc
        if g < CHOSEN // CHUNK - 1:
            top_ref[h] = jnp.broadcast_to(fresh, (MOST, 128))
            total_ref[h] = jnp.broadcast_to(total, (MOST, 128))
            acc_ref[h] = acc
        else:
            att[:, columns] = (acc / total).astype(BF16)

    def project_q():
        def tile(n, carry):
            columns = pl.ds(pl.multiple_of(n * 256, 256), 256)
            weights = wqo[0, :, :, :, columns].reshape(D, 256)
            piece = jnp.dot(normed[...], weights, preferred_element_type=F32)
            query[:, columns] = (piece * HEAD_DIM ** (-0.5)).astype(BF16)
            return carry

        lax.fori_loop(0, QW // 256, tile, 0)

    for g in range(CHOSEN // CHUNK + 1):
        if g == 0:
            by_core(zk_steps[0:1], xk_steps[0:1])
            y_last(0)
            project_q()
        if g == 2:
            y_second(1)

        def together(i, carry):
            if g < CHOSEN // CHUNK:
                for j in range(1 if g == 0 else 0, PER):

                    @pl.when(i == j)
                    def _():
                        n = g * PER + j
                        by_core(zk_steps[n : n + 1], xk_steps[n : n + 1])

            if g > 0:
                attend(g - 1, i)
            return carry

        lax.fori_loop(0, PER, together, 0)
        if g == 3:
            y_third(1)

    y_last(1)

    def project_out(n, carry):
        columns = pl.ds(pl.multiple_of(n * 256, 256), 256)
        weights = wqo[1, pl.ds(n * 4, 4)].reshape(256, QW)
        out[:, columns] = lax.dot_general(
            att[...], weights, (((1,), (1,)), ((), ())), preferred_element_type=F32
        ).astype(BF16)
        return carry

    lax.fori_loop(0, D // 256, project_out, 0)

    for whole, sem in (
        (kvw.at[pl.ds(0, HALF * (SEQ - 1)), :], w_send),
        (kvw.at[pl.ds(0, HALF * SEQ), :], d_send),
        (wqo.at[:, pl.ds(0, SEQ - 1), 0], o_send),
        (kv_in.at[pl.ds(0, SEQ - 1)], a_send),
        (kv.at[pl.ds(0, ROWS * (SEQ - 1)), :], kv_send),
        (wqo.at[0, :, pl.ds(0, 3)], q_send),
        (wqo.at[1, :, pl.ds(0, 3)], y_send),
        (wqo.at[:, :, pl.ds(0, 4)], p_send),
    ):
        pltpu.make_async_copy(whole, whole, sem).wait()


def mix_kernel(tile, tokens, block_out, meta, mixed):
    i = pl.program_id(0)
    place = lax.broadcasted_iota(jnp.int32, (tile, MOST), 0) + i * tile
    hit = place.astype(F32) == meta[0:1, :]
    gate = jnp.sum(jnp.where(hit, meta[1:2, :], 0.0), axis=1, keepdims=True)
    chosen_row = jnp.where(hit, 1.0, 0.0).astype(BF16)
    for n in range(D // 256):
        columns = slice(n * 256, (n + 1) * 256)
        rows = jnp.dot(chosen_row, block_out[:, columns], preferred_element_type=F32)
        mixed[:, columns] = (tokens[:, columns].astype(F32) + gate * rows).astype(BF16)


def per_device(tokens, chosen, gates, w_query, w_key, w_value, w_out):
    spots = chosen.astype(F32)
    c2 = spots.reshape(ROWS, SEQ)
    anywhere = pl.BlockSpec(memory_space=pl.ANY)
    inside = pl.BlockSpec(memory_space=pltpu.VMEM)
    dma = pltpu.SemaphoreType.DMA
    vmem = pltpu.VMEM
    block_out, meta = pl.pallas_call(
        block_kernel,
        out_shape=(
            jax.ShapeDtypeStruct((MOST, D), BF16),
            jax.ShapeDtypeStruct((8, MOST), F32),
        ),
        in_specs=[anywhere] * 5 + [inside] * 4,
        out_specs=(inside, inside),
        scratch_shapes=[
            vmem((TOK, D), BF16),
            vmem((D, 2 * KW), BF16),
            vmem((2, SEQ, PARTS, PIECE, QW), BF16),
            vmem((MOST, D), BF16),
            vmem((MOST, TOK), BF16),
            vmem((MOST, MOST), BF16),
            vmem((ROWS, MOST), BF16),
            vmem((MOST, CHOSEN), F32),
            vmem((MOST, QW), BF16),
            vmem((MOST, QW), BF16),
            vmem((MOST, 2 * KW), BF16),
            vmem((SEQ, SLOTS, 2 * KW), BF16),
            vmem((SEQ, SLOTS, 2 * KW), BF16),
            vmem((CHOSEN, 2 * KW), BF16),
            vmem((2, MOST, 128), F32),
            vmem((MOST, 128), F32),
            vmem((HEADS, MOST, 128), F32),
            vmem((HEADS, MOST, 128), F32),
            vmem((HEADS, MOST, 128), F32),
            dma((4,)),
            dma,
            dma,
            dma((SEQ,)),
            dma,
            dma((SEQ,)),
            dma,
            dma,
            dma,
            dma,
            dma,
            dma((SEQ,)),
            dma,
            dma((3, SEQ)),
            dma,
            dma((2, 4)),
            dma,
            dma((2,)),
        ],
        compiler_params=pltpu.CompilerParams(
            collective_id=0, has_side_effects=True, vmem_limit_bytes=56 * 1024 * 1024
        ),
        name="block",
    )(
        tokens,
        w_query.reshape(PARTS, PIECE, QW),
        w_key,
        w_value,
        w_out.T.reshape(PARTS, PIECE, QW),
        spots.reshape(1, CHOSEN),
        gates.reshape(1, CHOSEN),
        c2,
        c2.T,
    )
    tile = 256
    return pl.pallas_call(
        functools.partial(mix_kernel, tile),
        grid=(TOK // tile,),
        out_shape=jax.ShapeDtypeStruct((TOK, D), BF16),
        in_specs=[
            pl.BlockSpec((tile, D), lambda i: (i, 0)),
            pl.BlockSpec((MOST, D), lambda i: (0, 0)),
            pl.BlockSpec((8, MOST), lambda i: (0, 0)),
        ],
        out_specs=pl.BlockSpec((tile, D), lambda i: (i, 0)),
        name="mix",
    )(tokens, block_out, meta)


def solution(mesh):
    return jax.shard_map(
        per_device,
        mesh=mesh,
        in_specs=(
            P(("dp", "seq"), None),
            P("dp"),
            P("dp"),
            P("seq", None),
            P("seq", None),
            P("seq", None),
            P(None, "seq"),
        ),
        out_specs=P(("dp", "seq"), None),
        check_vma=False,
    )
```

time: 130 us -> 114 us (0.88)
  Pallas kernels: 125 us -> 112 us
  local copies, waits for them, and re-layouts: 2.5 us -> 0.77 us
    pallas_call x1, Pallas kernels: 119 us -> 107 us  [per_device(): pl.pallas_call(block_kernel, out_shape=(jax.ShapeDtypeStruct((MOST, D), B...]
    unnamed x5 -> x4, local copies, waits for them, and re-layouts: 1.75 us -> 0.01 us
where the time goes in v2:
time: 114 us
  Pallas kernels  112 us (98%)
    pallas_call x1, Pallas kernels, per_device(): pl.pallas_call(block_kernel, out_shape=(jax.ShapeDtypeStruct((MOST, D), B...  107 us
    pallas_call x1, Pallas kernels, per_device(): pl.pallas_call(functools.partial(mix_kernel, tile), grid=(TOK // tile,),...  5.93 us

profile of v2, /device:TPU:8, one launch (start us, length us, event | category | flops | bytes accessed | tf_op | source)
XLA Modules:
  0.0 113.9 jit_solution(14423876652969803591)
XLA Ops:
  0.0 0.7 convert_element_type.3
  0.7 0.0 copy-start.1
  0.7 0.1 reshape.19.c2
  0.8 0.0 copy-start
  0.8 0.7 copy.9
  1.5 0.0 copy-done.1
  1.5 0.0 copy-done
  1.5 106.5 %block.1 = (bf16[256,2048]{1,0:T(8,128)(2,1)}, f32[8,256]{1,0:T(8,128)}) custom-call(bf16[1024,2048]{1,0:T(8,128)(2,1)} %tokens.3, bf16[8,8,1024]{2,1,0:T(8,128)(2,1)} %bitcast.8, bf16[64,256]{1,0:T(8,128)(2,1)} %wk.1, bf16[64,256]{1,0:T(8,128)(2,1)} %wv.1, bf16[8,8,1024]{2,1,0:T(8,128)(2,1)} %bitcast.9, f32[1,4096]{1,0:T(1,128)} %bitcast.7, ...), custom_call_target="tpu_custom_call" | custom-call | tf_op jit(solution)/shard_map/block/pallas_call | solution.py:488
  108.0 5.9 %mix.1 = bf16[1024,2048]{1,0:T(8,128)(2,1)} custom-call(bf16[1024,2048]{1,0:T(8,128)(2,1)} %tokens.3, bf16[256,2048]{1,0:T(8,128)(2,1)} %get-tuple-element.7.block_out, f32[8,256]{1,0:T(8,128)} %get-tuple-element.8.meta), custom_call_target="tpu_custom_call" | custom-call | tf_op jit(solution)/shard_map/mix/pallas_call | solution.py:551
Async XLA Ops:
  0.7 0.8 copy-start.1
  0.8 0.7 copy-start

commit v3 on v2

v3 whole, which is shorter than its diff:
```python
import functools

import jax
import jax.numpy as jnp
from jax import lax
from jax.experimental import pallas as pl
from jax.experimental.pallas import tpu as pltpu
from jax.sharding import PartitionSpec as P

HEADS = 8
KV_HEADS = 2
GROUP = HEADS // KV_HEADS
HEAD_DIM = 128
D = 2048
QW = HEADS * HEAD_DIM
KW = KV_HEADS * HEAD_DIM
SEQ = 32
NX = 4
NZ = 8
TOK = 1024
CHOSEN = 4096
ROWS = 128
MOST = 256
SLOTS = 8
DEPTH = D // SEQ
HALF = DEPTH // 2
PARTS = 8
PIECE = DEPTH // PARTS
CHUNK = 1024
PER = CHUNK // ROWS
SIDE = ROWS // 2
EARLY = 5
PAIR = 2
TILE = 256
TILES = TOK // TILE
MESH = pl.DeviceIdType.MESH
F32 = jnp.float32
BF16 = jnp.bfloat16
FAR = -1e30


def ring_groups(na, nb):
    columns = [0]
    for k in range(1, na // 2 + 1):
        columns += [-k, k] if k < na // 2 else [-k]
    groups = [[(0, 0)]] + [[(j, 0)] for j in columns[1:]]
    for m in range(1, nb // 2):
        groups += [[(j, -m), (j, m)] for j in columns]
    return groups + [[(j, far_side(n) * -(nb // 2)) for n, j in enumerate(columns)]], columns


def far_side(order):
    return 1 if order % 2 == 0 else -1


def ring_steps(na, nb, direct, send, wait):
    groups, columns = ring_groups(na, nb)

    def first():
        along = [(-p, 0) for p in columns[1:]] if direct else [(1, 0), (-1, 0)]
        for to in along + [(0, 1), (0, -1)]:
            send((0, 0), to)

    def step(index):
        wait(index)
        for j, m in groups[index]:
            if m == 0:
                side = -1 if j > 0 else 1
                if not direct and abs(j) < (na // 2 if side == 1 else na // 2 - 1):
                    send((j, m), (side, 0))
                send((j, m), (0, 1))
                send((j, m), (0, -1))
            else:
                side = -1 if m > 0 else 1
                reach = nb // 2 if side == far_side(columns.index(j)) else nb // 2 - 1
                if abs(m) < reach:
                    send((j, m), (0, side))

    return [first] + [functools.partial(step, n) for n in range(1, len(groups))]


def places(na, nb):
    flat = {}
    for index, group in enumerate(ring_groups(na, nb)[0]):
        for j, m in group:
            flat[j % na, m % nb] = (len(flat), index)
    return flat


def block_kernel(
    tokens, wq, wk, wv, wo, crow, grow, listed_in,
    out, meta_out,
    out_tile, meta, tok, kvw, wqo, normed, onehot, deal, take, bias, query, att, kv_own, kv_slots, kv_in, kv,
    cpos, spots_f, c2t, wide, top_ref, total_ref, acc_ref,
    load_sem, tok_sem, out_sem, w_send, w_recv, o_send, o_recv, d_send, d_recv, a_send, a_recv,
    kv_send, kv_recv, q_send, q_recv, y_send, y_recv, p_send, p_recv,
):
    dp = lax.axis_index("dp")
    me = lax.axis_index("seq")
    core = lax.rem(dp, 2)
    y = dp // 2
    partner = dp + 1 - 2 * core
    x, z = me // NZ, lax.rem(me, NZ)

    def along_y(k):
        return lax.rem(y + k + 4, 4) * 2 + core

    def zf(block):
        return lax.rem(x + block[1] + NX, NX) * NZ + lax.rem(z + block[0] + NZ, NZ)

    def xf(block):
        return lax.rem(x + block[0] + NX, NX) * NZ + lax.rem(z + block[1] + NZ, NZ)

    def remote(src, dst, send_sem, recv_sem, to_dp, to_seq):
        return pltpu.make_async_remote_copy(
            src_ref=src,
            dst_ref=dst,
            send_sem=send_sem,
            recv_sem=recv_sem,
            device_id=(to_dp, to_seq),
            device_id_type=MESH,
        )

    def kv_unit(s, half):
        start = s * DEPTH + half * HALF
        return pl.ds(pl.multiple_of(start, HALF), HALF)

    own = kv_unit(me, core)
    loads = [
        pltpu.make_async_copy(wk.at[pl.ds(core * HALF, HALF), :], kvw.at[own, 0:KW], load_sem.at[0]),
        pltpu.make_async_copy(wv.at[pl.ds(core * HALF, HALF), :], kvw.at[own, KW : 2 * KW], load_sem.at[1]),
        pltpu.make_async_copy(wq.at[dp], wqo.at[0, me, dp], load_sem.at[2]),
        pltpu.make_async_copy(wo.at[dp], wqo.at[1, me, dp], load_sem.at[3]),
    ]
    for copy in loads:
        copy.start()
    token_load = pltpu.make_async_copy(tokens, tok, tok_sem)
    token_load.start()

    barrier = pltpu.get_barrier_semaphore()

    def greet(j, carry):
        pl.semaphore_signal(
            barrier, inc=1, device_id=(dp, lax.rem(me + j, SEQ)), device_id_type=MESH
        )
        return carry

    lax.fori_loop(1, SEQ, greet, 0)
    for other in (partner, along_y(1), along_y(-1)):
        pl.semaphore_signal(barrier, inc=1, device_id=(other, me), device_id_type=MESH)

    base = (me * TOK).astype(F32)
    listed = crow[...].astype(F32)
    spots_f[...] = listed
    first = jnp.sum(jnp.where(listed < base, 1.0, 0.0), axis=1, keepdims=True)
    last = jnp.sum(jnp.where(listed < base + TOK, 1.0, 0.0), axis=1, keepdims=True)
    shift = jnp.minimum(first, float(CHOSEN - MOST))

    def pick(i, carry):
        rows = pl.ds(pl.multiple_of(i * 32, 32), 32)
        lane = lax.broadcasted_iota(jnp.int32, (32, CHOSEN), 1).astype(F32)
        rank = lax.broadcasted_iota(jnp.int32, (32, 1), 0).astype(F32)
        hit = lane == rank + (shift + (i * 32).astype(F32))
        spot = jnp.sum(jnp.where(hit, spots_f[...], 0.0), axis=1, keepdims=True)
        gate = jnp.sum(jnp.where(hit, grow[...], 0.0), axis=1, keepdims=True)
        cpos[0, rows, :] = jnp.broadcast_to(spot, (32, 128))
        cpos[1, rows, :] = jnp.broadcast_to(gate, (32, 128))
        return carry

    lax.fori_loop(0, MOST // 32, pick, 0)
    place = lax.broadcasted_iota(jnp.int32, (MOST, TOK), 1).astype(F32)
    onehot[...] = jnp.where(place == cpos[0, :, 0:1] - base, 1.0, 0.0).astype(BF16)

    for copy in loads:
        copy.wait()
    pl.semaphore_wait(barrier, SEQ + 2)

    z_places, x_places = places(NZ, NX), places(NX, NZ)
    z_blocks, x_blocks = list(z_places), list(x_places)

    def block_at(i):
        return zf(z_blocks[i])

    def q_copy(s, k, sem, to):
        piece = wqo.at[0, s, along_y(k)]
        return remote(piece, piece, q_send, q_recv.at[sem], along_y(to), me)

    def to_y(n):
        s = block_at(n)
        q_copy(s, 0, n // 2, 1).start()
        q_copy(s, 0, n // 2, -1).start()
        q_across(s, 0)

    def q_across(s, k):
        piece = wqo.at[0, s, along_y(k)]
        remote(piece, piece, p_send, p_recv.at[0], partner, me).start()

    def from_y(i):
        both = wqo.at[0, pl.ds(0, 4), 0]
        pltpu.make_async_copy(both, both, q_recv.at[i]).wait()
        low, high = block_at(2 * i), block_at(2 * i + 1)
        q_copy(low, -1, SEQ // 2, 1).start()
        q_copy(high, 1, SEQ // 2, -1).start()
        for s in (low, high):
            q_across(s, -1)
            q_across(s, 1)

    def first_gather(view, many, send_sem, recv_sem, arrived):
        groups = ring_groups(NZ, NX)[0]

        def send(block, to):
            group = z_places[(block[0] - to[0]) % NZ, (block[1] - to[1]) % NX][1]
            s = zf(block)
            remote(view(s), view(s), send_sem, recv_sem.at[group], dp, zf(to)).start()

        def wait(index):
            some = many(len(groups[index]))
            pltpu.make_async_copy(some, some, recv_sem.at[index]).wait()

        def then(index, step):
            step()
            for block in groups[index]:
                arrived(z_places[block[0] % NZ, block[1] % NX][0])

        steps = ring_steps(NZ, NX, True, send, wait)
        return [functools.partial(then, index, step) for index, step in enumerate(steps)]

    def kv_half(s):
        return kvw.at[kv_unit(s, core), :]

    def to_partner(n):
        half = kv_half(block_at(n))
        remote(half, half, d_send, d_recv, partner, me).start()

    w_steps = first_gather(
        kv_half, lambda n: kvw.at[pl.ds(0, n * HALF), :], w_send, w_recv, to_partner
    )
    o_steps = first_gather(
        lambda s: wqo.at[:, s, dp], lambda n: wqo.at[:, pl.ds(0, n), 0], o_send, o_recv, to_y
    )

    def gather_rows(n):
        columns = slice(n * 256, (n + 1) * 256)
        part = jnp.dot(onehot[...], tok[:, columns], preferred_element_type=F32)
        normed[:, columns] = part.astype(BF16)
        square = jnp.broadcast_to(jnp.sum(part * part, axis=1, keepdims=True), (MOST, 128))
        wide[...] = square if n == 0 else wide[...] + square

    def normalize(n):
        columns = slice(n * 512, (n + 1) * 512)
        scale = lax.rsqrt(wide[:, 0:1] * (1.0 / D) + 1e-06)
        normed[:, columns] = (normed[:, columns].astype(F32) * scale).astype(BF16)

    def place_rows():
        order = lax.broadcasted_iota(jnp.int32, (MOST, MOST), 1)
        slot = lax.broadcasted_iota(jnp.int32, (MOST, MOST), 0)
        rank = order + shift.astype(jnp.int32)
        offset = rank - first.astype(jnp.int32)
        inside = jnp.where(offset >= 0, 1, 0) * jnp.where(rank < last.astype(jnp.int32), 1, 0)
        goes = (rank & (SEQ - 1)) * SLOTS + (offset >> 5)
        deal[...] = jnp.where(goes == slot, inside, 0).astype(F32).astype(BF16)
        gate = cpos[1, :, 0:1]
        eye = order == slot
        meta[0:1, :] = jnp.sum(jnp.where(eye, cpos[0, :, 0:1] - base, 0.0), axis=0, keepdims=True)
        meta[1:2, :] = jnp.sum(jnp.where(eye, gate, 0.0), axis=0, keepdims=True)

    def dealt_order():
        rows = listed_in[...].astype(F32)
        r = lax.broadcasted_iota(jnp.int32, (SEQ, ROWS), 0)
        k = lax.broadcasted_iota(jnp.int32, (SEQ, ROWS), 1)
        for q in range(ROWS // SEQ):
            take_k = jnp.where(k == r * (ROWS // SEQ) + q, 1.0, 0.0)
            part = lax.dot_general(
                rows[:, q * SEQ : (q + 1) * SEQ], take_k, (((0,), (0,)), ((), ())),
                precision=lax.Precision.HIGHEST, preferred_element_type=F32,
            )
            c2t[...] = part if q == 0 else c2t[...] + part

    def find_slots():
        lane32 = lax.broadcasted_iota(jnp.int32, (ROWS, SEQ), 1)
        mine = jnp.sum(jnp.where(lane32 == me, c2t[...].T, 0.0), axis=1, keepdims=True)
        source = jnp.floor(mine * (1.0 / TOK))

        def before(i, total):
            columns = pl.ds(pl.multiple_of(i * 512, 512), 512)
            return total + jnp.sum(
                jnp.where(spots_f[:, columns] < source * TOK, 1.0, 0.0), axis=1, keepdims=True
            )

        starts = lax.fori_loop(0, CHOSEN // 512, before, jnp.zeros((ROWS, 1), F32))
        my_rank = lax.broadcasted_iota(jnp.int32, (ROWS, 1), 0).astype(F32) * SEQ + me.astype(F32)
        found = source * SLOTS + jnp.floor((my_rank - starts) * (1.0 / SEQ))
        take[...] = jnp.where(
            lax.broadcasted_iota(jnp.int32, (ROWS, MOST), 1).astype(F32) == found, 1.0, 0.0
        ).astype(BF16)

    def bias_blocks(low, high):
        for slot in range(low, high):
            spots = jnp.where(
                lax.broadcasted_iota(jnp.int32, (1, ROWS), 1) < SIDE,
                c2t[pl.ds(zf(z_blocks[slot]), 1), :],
                c2t[pl.ds(xf(x_blocks[slot]), 1), :],
            )
            bias[:, slot * ROWS : (slot + 1) * ROWS] = jnp.where(
                spots <= cpos[0, :, 0:1], 0.0, FAR
            )

    work = [functools.partial(gather_rows, n) for n in range(D // 256)]
    work += [functools.partial(normalize, n) for n in range(D // 512)]
    work += [dealt_order, place_rows, find_slots]
    work += [functools.partial(bias_blocks, n, n + 4) for n in range(0, SEQ, 4)]

    w_steps[0]()
    token_load.wait()
    done = 0
    for i in range(1, len(w_steps)):
        until = len(work) * i // (len(w_steps) - 1)
        for item in work[done:until]:
            item()
        done = until
        w_steps[i]()
        if i == NZ - 1:
            o_steps[0]()
        if i >= NZ + 1 and i - NZ < NZ:
            o_steps[i - NZ]()

    def part(a, k, low=0, high=SEQ):
        return wqo.at[a, pl.ds(low, high - low), along_y(k)]

    def along(a, k, slot, to, low=0, high=SEQ):
        return remote(
            part(a, k, low, high), part(a, k, low, high), y_send, y_recv.at[a, slot], along_y(to), me
        )

    def across(a, k):
        remote(part(a, k), part(a, k), p_send, p_recv.at[a], partner, me).start()

    def y_first(a):
        along(a, 0, 0, 1).start()
        along(a, 0, 1, -1).start()
        across(a, 0)

    def y_second(a):
        along(a, -1, 0, 1).wait_recv()
        along(a, -1, 2, 1, 0, SEQ // 2).start()
        across(a, -1)
        along(a, 1, 1, -1).wait_recv()
        along(a, 1, 3, -1, SEQ // 2, SEQ).start()
        across(a, 1)

    def y_third(a):
        along(a, 2, 2, 1, 0, SEQ // 2).wait_recv()
        along(a, 2, 3, -1, SEQ // 2, SEQ).wait_recv()
        across(a, 2)

    def y_last(a):
        whole = wqo.at[a, :, pl.ds(0, 4)]
        pltpu.make_async_copy(whole, whole, p_recv.at[a]).wait()

    whole = kvw.at[pl.ds(0, HALF * SEQ), :]
    pltpu.make_async_copy(whole, whole, d_recv).wait()

    for n in range(2):
        columns = slice(n * 256, (n + 1) * 256)
        kv_own[:, columns] = jnp.dot(
            normed[...], kvw[:, columns], preferred_element_type=F32
        ).astype(BF16)
    leaving = jnp.dot(deal[...], kv_own[...], preferred_element_type=F32)
    kv_slots[...] = leaving.reshape(SEQ, SLOTS, 2 * KW).astype(BF16)

    def send_slot(j, carry):
        dest = lax.rem(me + j, SEQ)
        remote(kv_slots.at[dest], kv_in.at[me], a_send, a_recv, dp, dest).start()
        return carry

    lax.fori_loop(1, SEQ, send_slot, 0)
    kv_in[me] = kv_slots[me]

    for i in range(NZ, len(o_steps)):
        o_steps[i]()
    for i in range(EARLY):
        from_y(i)

    whole = kv_in.at[pl.ds(0, SEQ - 1)]
    pltpu.make_async_copy(whole, whole, a_recv).wait()
    came = kv_in[...].astype(F32).reshape(MOST, 2 * KW).astype(BF16)
    kv[0:ROWS, :] = jnp.dot(take[...], came, preferred_element_type=F32).astype(BF16)

    def second_gather(route, at, na, nb, order):
        groups = ring_groups(na, nb)[0]

        def rows(n):
            return kv.at[pl.ds(n * ROWS + route * SIDE, SIDE), :]

        def send(block, to):
            n = order[block[0] % na, block[1] % nb][0]
            lands, group = order[(block[0] - to[0]) % na, (block[1] - to[1]) % nb]
            remote(rows(n), rows(lands), kv_send, kv_recv.at[route, group], dp, at(to)).start()

        def wait(index):
            some = kv.at[pl.ds(0, len(groups[index]) * SIDE), :]
            pltpu.make_async_copy(some, some, kv_recv.at[route, index]).wait()

        return ring_steps(na, nb, False, send, wait)

    z_steps = second_gather(0, zf, NZ, NX, z_places)
    x_steps = second_gather(1, xf, NX, NZ, x_places)

    def attend(g, pair):
        e = pair // (GROUP // PAIR)
        rows = slice(g * CHUNK, (g + 1) * CHUNK)
        keys = kv[rows, pl.ds(pl.multiple_of(e * HEAD_DIM, HEAD_DIM), HEAD_DIM)]
        values = kv[rows, pl.ds(pl.multiple_of(KW + e * HEAD_DIM, HEAD_DIM), HEAD_DIM)]
        heads = [pair * PAIR + n for n in range(PAIR)]
        columns = [pl.ds(pl.multiple_of(h * HEAD_DIM, HEAD_DIM), HEAD_DIM) for h in heads]
        scores = [
            lax.dot_general(
                query[:, c], keys, (((1,), (1,)), ((), ())), preferred_element_type=F32
            )
            for c in columns
        ]
        for h, c, score in zip(heads, columns, scores):
            score = score + bias[:, rows]
            fresh = jnp.max(score, axis=1, keepdims=True)
            if g > 0:
                before = top_ref[h][:, 0:1]
                fresh = jnp.maximum(before, fresh)
            probs = jnp.exp(score - fresh)
            total = jnp.sum(probs, axis=1, keepdims=True)
            acc = jnp.dot(probs.astype(BF16), values, preferred_element_type=F32)
            if g > 0:
                shrink = jnp.exp(before - fresh)
                total = total_ref[h][:, 0:1] * shrink + total
                acc = acc_ref[h] * shrink + acc
            if g < CHOSEN // CHUNK - 1:
                top_ref[h] = jnp.broadcast_to(fresh, (MOST, 128))
                total_ref[h] = jnp.broadcast_to(total, (MOST, 128))
                acc_ref[h] = acc
            else:
                att[:, c] = (acc / total).astype(BF16)

    def project_q():
        def tile(n, carry):
            columns = pl.ds(pl.multiple_of(n * 256, 256), 256)
            weights = wqo[0, :, :, :, columns].reshape(D, 256)
            piece = jnp.dot(normed[...], weights, preferred_element_type=F32)
            query[:, columns] = (piece * HEAD_DIM ** (-0.5)).astype(BF16)
            return carry

        lax.fori_loop(0, QW // 256, tile, 0)

    def last_of_y():
        y_first(1)
        whole = wqo.at[0, :, 0]
        pltpu.make_async_copy(whole, whole, q_recv.at[SEQ // 2]).wait()
        across(0, 2)

    z_steps[0]()
    x_steps[0]()
    for i in range(EARLY, SEQ // 2):
        from_y(i)
        if i == 9:
            z_steps[1]()
            x_steps[1]()
            z_steps[2]()
            x_steps[2]()
        if i == 14:
            x_steps[3]()
            z_steps[3]()
            z_steps[4]()
    last_of_y()
    x_steps[4]()
    z_steps[5]()
    z_steps[6]()
    y_last(0)
    project_q()
    x_steps[5]()
    z_steps[7]()

    windows = {
        1: [[z_steps[n + 8], x_steps[n + 6]] for n in range(4)],
        2: [[z_steps[n + 12], x_steps[n + 10]] for n in range(4)],
        3: [[x_steps[14]], [x_steps[15]], [z_steps[16]], [x_steps[16]]],
    }
    for g in range(1, CHOSEN // CHUNK):
        if g == 3:
            y_second(1)

        def together(i, carry):
            for j in range(HEADS // PAIR):

                @pl.when(i == j)
                def _():
                    for step in windows[g][j]:
                        step()

            attend(g - 1, i)
            return carry

        lax.fori_loop(0, HEADS // PAIR, together, 0)

    def alone(i, carry):
        attend(CHOSEN // CHUNK - 1, i)
        return carry

    lax.fori_loop(0, HEADS // PAIR, alone, 0)
    y_third(1)
    y_last(1)

    def project_out(n, carry):
        columns = pl.ds(pl.multiple_of(n * 256, 256), 256)
        weights = wqo[1, pl.ds(n * 4, 4)].reshape(256, QW)
        out_tile[n] = lax.dot_general(
            att[...], weights, (((1,), (1,)), ((), ())), preferred_element_type=F32
        ).astype(BF16)
        pltpu.make_async_copy(out_tile.at[n], out.at[n], out_sem.at[0]).start()
        return carry

    meta_copy = pltpu.make_async_copy(meta, meta_out, out_sem.at[1])
    meta_copy.start()
    lax.fori_loop(0, D // 256, project_out, 0)

    for whole, sem in (
        (kvw.at[pl.ds(0, HALF * (SEQ - 1)), :], w_send),
        (kvw.at[pl.ds(0, HALF * SEQ), :], d_send),
        (wqo.at[:, pl.ds(0, SEQ - 1), 0], o_send),
        (kv_in.at[pl.ds(0, SEQ - 1)], a_send),
        (kv.at[pl.ds(0, ROWS * (SEQ - 1)), :], kv_send),
        (wqo.at[0, :, pl.ds(0, 3)], q_send),
        (wqo.at[1, :, pl.ds(0, 3)], y_send),
        (wqo.at[:, :, pl.ds(0, 4)], p_send),
    ):
        pltpu.make_async_copy(whole, whole, sem).wait()
    meta_copy.wait()
    pltpu.make_async_copy(out_tile, out, out_sem.at[0]).wait()


def mix_kernel(tokens, block_out, meta, mixed, tok, rows_in, result, load_sem, rows_sem, store_sem):
    def load(n):
        return pltpu.make_async_copy(tokens.at[n], tok.at[n], load_sem.at[n])

    def store(n):
        return pltpu.make_async_copy(result.at[n], mixed.at[n], store_sem.at[n])

    rows_load = pltpu.make_async_copy(block_out, rows_in, rows_sem)
    rows_load.start()
    for n in range(TILES):
        load(n).start()
    rows_load.wait()

    def tile(n, carry):
        place = lax.broadcasted_iota(jnp.int32, (TILE, MOST), 0) + n * TILE
        hit = place.astype(F32) == meta[0:1, :]
        high = meta[1:2, :].astype(BF16).astype(F32)
        low = meta[1:2, :] - high
        lift_high = jnp.where(hit, high, 0.0).astype(BF16)
        lift_low = jnp.where(hit, low, 0.0).astype(BF16)
        load(n).wait()
        for c in range(D // 256):
            columns = slice(c * 256, (c + 1) * 256)
            rows = jnp.dot(lift_high, rows_in[c], preferred_element_type=F32)
            rows = rows + jnp.dot(lift_low, rows_in[c], preferred_element_type=F32)
            result[n, :, columns] = (tok[n, :, columns].astype(F32) + rows).astype(BF16)
        store(n).start()
        return carry

    lax.fori_loop(0, TILES, tile, 0)
    for n in range(TILES):
        store(n).wait()


def per_device(tokens, chosen, gates, w_query, w_key, w_value, w_out):
    anywhere = pl.BlockSpec(memory_space=pl.ANY)
    inside = pl.BlockSpec(memory_space=pltpu.VMEM)
    dma = pltpu.SemaphoreType.DMA
    vmem = pltpu.VMEM
    block_out, meta = pl.pallas_call(
        block_kernel,
        out_shape=(
            jax.ShapeDtypeStruct((D // 256, MOST, 256), BF16),
            jax.ShapeDtypeStruct((8, MOST), F32),
        ),
        in_specs=[anywhere] * 5 + [inside] * 3,
        out_specs=(anywhere, anywhere),
        scratch_shapes=[
            vmem((D // 256, MOST, 256), BF16),
            vmem((8, MOST), F32),
            vmem((TOK, D), BF16),
            vmem((D, 2 * KW), BF16),
            vmem((2, SEQ, PARTS, PIECE, QW), BF16),
            vmem((MOST, D), BF16),
            vmem((MOST, TOK), BF16),
            vmem((MOST, MOST), BF16),
            vmem((ROWS, MOST), BF16),
            vmem((MOST, CHOSEN), F32),
            vmem((MOST, QW), BF16),
            vmem((MOST, QW), BF16),
            vmem((MOST, 2 * KW), BF16),
            vmem((SEQ, SLOTS, 2 * KW), BF16),
            vmem((SEQ, SLOTS, 2 * KW), BF16),
            vmem((CHOSEN, 2 * KW), BF16),
            vmem((2, MOST, 128), F32),
            vmem((1, CHOSEN), F32),
            vmem((SEQ, ROWS), F32),
            vmem((MOST, 128), F32),
            vmem((HEADS, MOST, 128), F32),
            vmem((HEADS, MOST, 128), F32),
            vmem((HEADS, MOST, 128), F32),
            dma((4,)),
            dma,
            dma((2,)),
            dma,
            dma((17,)),
            dma,
            dma((17,)),
            dma,
            dma,
            dma,
            dma,
            dma,
            dma((2, 17)),
            dma,
            dma((17,)),
            dma,
            dma((2, 4)),
            dma,
            dma((2,)),
        ],
        compiler_params=pltpu.CompilerParams(
            collective_id=0, has_side_effects=True, vmem_limit_bytes=56 * 1024 * 1024
        ),
        name="block",
    )(
        tokens,
        w_query.reshape(PARTS, PIECE, QW),
        w_key,
        w_value,
        w_out.T.reshape(PARTS, PIECE, QW),
        chosen.reshape(1, CHOSEN),
        gates.reshape(1, CHOSEN),
        chosen.reshape(SEQ, ROWS),
    )
    mixed = pl.pallas_call(
        mix_kernel,
        out_shape=jax.ShapeDtypeStruct((TILES, TILE, D), BF16),
        in_specs=[anywhere, anywhere, inside],
        out_specs=anywhere,
        scratch_shapes=[
            vmem((TILES, TILE, D), BF16),
            vmem((D // 256, MOST, 256), BF16),
            vmem((TILES, TILE, D), BF16),
            dma((TILES,)),
            dma,
            dma((TILES,)),
        ],
        compiler_params=pltpu.CompilerParams(vmem_limit_bytes=56 * 1024 * 1024),
        name="mix",
    )(tokens.reshape(TILES, TILE, D), block_out, meta)
    return mixed.reshape(TOK, D)


def solution(mesh):
    return jax.shard_map(
        per_device,
        mesh=mesh,
        in_specs=(
            P(("dp", "seq"), None),
            P("dp"),
            P("dp"),
            P("seq", None),
            P("seq", None),
            P("seq", None),
            P(None, "seq"),
        ),
        out_specs=P(("dp", "seq"), None),
        check_vma=False,
    )
```

time: 114 us -> 98.1 us (0.86)
  the two profiles are of different devices: /device:TPU:8 before, /device:TPU:1 now
where the time goes in v3:
time: 98.1 us; the launch traced here: 97.8 us
  Pallas kernels  97.8 us (100%)
    pallas_call x1, Pallas kernels, per_device(): pl.pallas_call(block_kernel, out_shape=(jax.ShapeDtypeStruct((D // 256, M...  90.9 us
    pallas_call x1, Pallas kernels, per_device(): pl.pallas_call(mix_kernel, out_shape=jax.ShapeDtypeStruct((TILES, TILE, D...  6.96 us

profile of v3, /device:TPU:1, one launch (start us, length us, event | category | flops | bytes accessed | tf_op | source)
XLA Modules:
  0.0 97.8 jit_solution(12155979713010596759)
XLA Ops:
  0.0 90.9 %block.1 = (bf16[8,256,256]{2,1,0:T(8,128)(2,1)}, f32[8,256]{1,0:T(8,128)}) custom-call(bf16[1024,2048]{1,0:T(8,128)(2,1)} %tokens.1, bf16[8,8,1024]{2,1,0:T(8,128)(2,1)} %bitcast.10, bf16[64,256]{1,0:T(8,128)(2,1)} %wk.1, bf16[64,256]{1,0:T(8,128)(2,1)} %wv.1, bf16[8,8,1024]{2,1,0:T(8,128)(2,1)} %bitcast.11, s32[1,4096]{1,0:T(1,128)} %bitcast.12, ...), custom_call_target="tpu_custom_call" | custom-call | tf_op jit(solution)/shard_map/block/pallas_call | solution.py:577
  90.9 7.0 %mix.1 = bf16[4,256,2048]{2,1,0:T(8,128)(2,1)} custom-call(bf16[4,256,2048]{2,1,0:T(8,128)(2,1)} %bitcast.9, bf16[8,256,256]{2,1,0:T(8,128)(2,1)} %get-tuple-element.7.block_out, f32[8,256]{1,0:T(8,128)} %get-tuple-element.8.meta), custom_call_target="tpu_custom_call" | custom-call | tf_op jit(solution)/shard_map/mix/pallas_call | solution.py:643

commit v4 on v3

--- a/solution.py
+++ b/solution.py
@@ -53,12 +53,13 @@
     return 1 if order % 2 == 0 else -1
 
 
-def ring_steps(na, nb, direct, send, wait):
+def ring_steps(na, nb, direct, far, send, wait):
     groups, columns = ring_groups(na, nb)
+    across = [(0, 1), (0, -1)] + ([(0, m) for m in range(2, nb - 1)] if far else [])
 
     def first():
         along = [(-p, 0) for p in columns[1:]] if direct else [(1, 0), (-1, 0)]
-        for to in along + [(0, 1), (0, -1)]:
+        for to in along + across:
             send((0, 0), to)
 
     def step(index):
@@ -68,9 +69,9 @@
                 side = -1 if j > 0 else 1
                 if not direct and abs(j) < (na // 2 if side == 1 else na // 2 - 1):
                     send((j, m), (side, 0))
-                send((j, m), (0, 1))
-                send((j, m), (0, -1))
-            else:
+                for to in across:
+                    send((j, m), to)
+            elif not far:
                 side = -1 if m > 0 else 1
                 reach = nb // 2 if side == far_side(columns.index(j)) else nb // 2 - 1
                 if abs(m) < reach:
@@ -205,7 +206,7 @@
             q_across(s, -1)
             q_across(s, 1)
 
-    def first_gather(view, many, send_sem, recv_sem, arrived):
+    def first_gather(far, view, many, send_sem, recv_sem, arrived):
         groups = ring_groups(NZ, NX)[0]
 
         def send(block, to):
@@ -222,7 +223,7 @@
             for block in groups[index]:
                 arrived(z_places[block[0] % NZ, block[1] % NX][0])
 
-        steps = ring_steps(NZ, NX, True, send, wait)
+        steps = ring_steps(NZ, NX, True, far, send, wait)
         return [functools.partial(then, index, step) for index, step in enumerate(steps)]
 
     def kv_half(s):
@@ -233,10 +234,18 @@
         remote(half, half, d_send, d_recv, partner, me).start()
 
     w_steps = first_gather(
-        kv_half, lambda n: kvw.at[pl.ds(0, n * HALF), :], w_send, w_recv, to_partner
+        False,
+        kv_half, lambda n: kvw.at[pl.ds(0, n * HALF), :], w_send, w_recv, to_partner,
+    )
+    q_steps = first_gather(
+        True,
+        lambda s: wqo.at[0, s, dp], lambda n: wqo.at[0, pl.ds(0, n), 0],
+        o_send.at[0], o_recv.at[0], to_y,
     )
     o_steps = first_gather(
-        lambda s: wqo.at[:, s, dp], lambda n: wqo.at[:, pl.ds(0, n), 0], o_send, o_recv, to_y
+        True,
+        lambda s: wqo.at[1, s, dp], lambda n: wqo.at[1, pl.ds(0, n), 0],
+        o_send.at[1], o_recv.at[1], lambda n: None,
     )
 
     def gather_rows(n):
@@ -320,9 +329,13 @@
         done = until
         w_steps[i]()
         if i == NZ - 1:
+            q_steps[0]()
             o_steps[0]()
-        if i >= NZ + 1 and i - NZ < NZ:
-            o_steps[i - NZ]()
+
+    for n in range(1, NZ):
+        q_steps[n]()
+    for n in range(1, NZ):
+        o_steps[n]()
 
     def part(a, k, low=0, high=SEQ):
         return wqo.at[a, pl.ds(low, high - low), along_y(k)]
@@ -376,8 +389,8 @@
     lax.fori_loop(1, SEQ, send_slot, 0)
     kv_in[me] = kv_slots[me]
 
-    for i in range(NZ, len(o_steps)):
-        o_steps[i]()
+    for i in range(NZ, len(q_steps)):
+        q_steps[i]()
     for i in range(EARLY):
         from_y(i)
 
@@ -401,7 +414,7 @@
             some = kv.at[pl.ds(0, len(groups[index]) * SIDE), :]
             pltpu.make_async_copy(some, some, kv_recv.at[route, index]).wait()
 
-        return ring_steps(na, nb, False, send, wait)
+        return ring_steps(na, nb, False, False, send, wait)
 
     z_steps = second_gather(0, zf, NZ, NX, z_places)
     x_steps = second_gather(1, xf, NX, NZ, x_places)
@@ -468,13 +481,15 @@
             x_steps[3]()
             z_steps[3]()
             z_steps[4]()
-    last_of_y()
+    for i in range(NZ, len(o_steps)):
+        o_steps[i]()
     x_steps[4]()
     z_steps[5]()
     z_steps[6]()
+    last_of_y()
+    x_steps[5]()
     y_last(0)
     project_q()
-    x_steps[5]()
     z_steps[7]()
 
     windows = {
@@ -523,7 +538,8 @@
     for whole, sem in (
         (kvw.at[pl.ds(0, HALF * (SEQ - 1)), :], w_send),
         (kvw.at[pl.ds(0, HALF * SEQ), :], d_send),
-        (wqo.at[:, pl.ds(0, SEQ - 1), 0], o_send),
+        (wqo.at[0, pl.ds(0, SEQ - 1), 0], o_send.at[0]),
+        (wqo.at[1, pl.ds(0, SEQ - 1), 0], o_send.at[1]),
         (kv_in.at[pl.ds(0, SEQ - 1)], a_send),
         (kv.at[pl.ds(0, ROWS * (SEQ - 1)), :], kv_send),
         (wqo.at[0, :, pl.ds(0, 3)], q_send),
@@ -551,16 +567,14 @@
     def tile(n, carry):
         place = lax.broadcasted_iota(jnp.int32, (TILE, MOST), 0) + n * TILE
         hit = place.astype(F32) == meta[0:1, :]
-        high = meta[1:2, :].astype(BF16).astype(F32)
-        low = meta[1:2, :] - high
-        lift_high = jnp.where(hit, high, 0.0).astype(BF16)
-        lift_low = jnp.where(hit, low, 0.0).astype(BF16)
+        gate = jnp.sum(jnp.where(hit, meta[1:2, :], 0.0), axis=1, keepdims=True)
+        gate = jnp.broadcast_to(gate, (TILE, 256))
+        chosen_row = jnp.where(hit, 1.0, 0.0).astype(BF16)
         load(n).wait()
         for c in range(D // 256):
             columns = slice(c * 256, (c + 1) * 256)
-            rows = jnp.dot(lift_high, rows_in[c], preferred_element_type=F32)
-            rows = rows + jnp.dot(lift_low, rows_in[c], preferred_element_type=F32)
-            result[n, :, columns] = (tok[n, :, columns].astype(F32) + rows).astype(BF16)
+            rows = jnp.dot(chosen_row, rows_in[c], preferred_element_type=F32)
+            result[n, :, columns] = (tok[n, :, columns].astype(F32) + gate * rows).astype(BF16)
         store(n).start()
         return carry
 
@@ -611,8 +625,8 @@
             dma((2,)),
             dma,
             dma((17,)),
-            dma,
-            dma((17,)),
+            dma((2,)),
+            dma((2, 17)),
             dma,
             dma,
             dma,

time: 98.1 us -> 95.2 us (0.970)
  the two profiles are of different devices: /device:TPU:1 before, /device:TPU:8 now
where the time goes in v4:
time: 95.2 us; the launch traced here: 94.1 us
  Pallas kernels  94 us (99%)
    pallas_call x1, Pallas kernels, per_device(): pl.pallas_call(block_kernel, out_shape=(jax.ShapeDtypeStruct((D // 256, M...  87.8 us
    pallas_call x1, Pallas kernels, per_device(): pl.pallas_call(mix_kernel, out_shape=jax.ShapeDtypeStruct((TILES, TILE, D...  6.2 us

profile of v4, /device:TPU:8, one launch (start us, length us, event | category | flops | bytes accessed | tf_op | source)
XLA Modules:
  0.0 94.1 jit_solution(14310083394135598982)
XLA Ops:
  0.0 87.8 %block.1 = (bf16[8,256,256]{2,1,0:T(8,128)(2,1)}, f32[8,256]{1,0:T(8,128)}) custom-call(bf16[1024,2048]{1,0:T(8,128)(2,1)} %tokens.1, bf16[8,8,1024]{2,1,0:T(8,128)(2,1)} %bitcast.10, bf16[64,256]{1,0:T(8,128)(2,1)} %wk.1, bf16[64,256]{1,0:T(8,128)(2,1)} %wv.1, bf16[8,8,1024]{2,1,0:T(8,128)(2,1)} %bitcast.11, s32[1,4096]{1,0:T(1,128)} %bitcast.12, ...), custom_call_target="tpu_custom_call" | custom-call | tf_op jit(solution)/shard_map/block/pallas_call | solution.py:591
  87.9 6.2 %mix.1 = bf16[4,256,2048]{2,1,0:T(8,128)(2,1)} custom-call(bf16[4,256,2048]{2,1,0:T(8,128)(2,1)} %bitcast.9, bf16[8,256,256]{2,1,0:T(8,128)(2,1)} %get-tuple-element.7.block_out, f32[8,256]{1,0:T(8,128)} %get-tuple-element.8.meta), custom_call_target="tpu_custom_call" | custom-call | tf_op jit(solution)/shard_map/mix/pallas_call | solution.py:657

commit v5 on v4

--- a/solution.py
+++ b/solution.py
@@ -30,8 +30,8 @@
 PER = CHUNK // ROWS
 SIDE = ROWS // 2
 EARLY = 5
-PAIR = 2
-TILE = 256
+PAIR = 4
+TILE = 512
 TILES = TOK // TILE
 MESH = pl.DeviceIdType.MESH
 F32 = jnp.float32
@@ -316,8 +316,7 @@
 
     work = [functools.partial(gather_rows, n) for n in range(D // 256)]
     work += [functools.partial(normalize, n) for n in range(D // 512)]
-    work += [dealt_order, place_rows, find_slots]
-    work += [functools.partial(bias_blocks, n, n + 4) for n in range(0, SEQ, 4)]
+    work += [place_rows]
 
     w_steps[0]()
     token_load.wait()
@@ -391,8 +390,12 @@
 
     for i in range(NZ, len(q_steps)):
         q_steps[i]()
-    for i in range(EARLY):
-        from_y(i)
+    dealt_order()
+    find_slots()
+    for n in range(8):
+        bias_blocks(4 * n, 4 * n + 4)
+        if n < EARLY:
+            from_y(n)
 
     whole = kv_in.at[pl.ds(0, SEQ - 1)]
     pltpu.make_async_copy(whole, whole, a_recv).wait()
@@ -497,6 +500,7 @@
         2: [[z_steps[n + 12], x_steps[n + 10]] for n in range(4)],
         3: [[x_steps[14]], [x_steps[15]], [z_steps[16]], [x_steps[16]]],
     }
+    windows = {g: [w[0] + w[1], w[2] + w[3]] for g, w in windows.items()}
     for g in range(1, CHOSEN // CHUNK):
         if g == 3:
             y_second(1)
@@ -555,8 +559,11 @@
     def load(n):
         return pltpu.make_async_copy(tokens.at[n], tok.at[n], load_sem.at[n])
 
-    def store(n):
-        return pltpu.make_async_copy(result.at[n], mixed.at[n], store_sem.at[n])
+    def store(n, half):
+        columns = slice(half * 1024, (half + 1) * 1024)
+        return pltpu.make_async_copy(
+            result.at[n, :, columns], mixed.at[n, :, columns], store_sem.at[half, n]
+        )
 
     rows_load = pltpu.make_async_copy(block_out, rows_in, rows_sem)
     rows_load.start()
@@ -575,12 +582,14 @@
             columns = slice(c * 256, (c + 1) * 256)
             rows = jnp.dot(chosen_row, rows_in[c], preferred_element_type=F32)
             result[n, :, columns] = (tok[n, :, columns].astype(F32) + gate * rows).astype(BF16)
-        store(n).start()
+            if c % 4 == 3:
+                store(n, c // 4).start()
         return carry
 
     lax.fori_loop(0, TILES, tile, 0)
     for n in range(TILES):
-        store(n).wait()
+        for half in range(2):
+            store(n, half).wait()
 
 
 def per_device(tokens, chosen, gates, w_query, w_key, w_value, w_out):
@@ -665,7 +674,7 @@
             vmem((TILES, TILE, D), BF16),
             dma((TILES,)),
             dma,
-            dma((TILES,)),
+            dma((2, TILES)),
         ],
         compiler_params=pltpu.CompilerParams(vmem_limit_bytes=56 * 1024 * 1024),
         name="mix",

time: 95.2 us -> 93.9 us (0.986)
  Pallas kernels: 94 us -> 92.4 us
where the time goes in v5:
time: 93.9 us; the launch traced here: 92.5 us
  Pallas kernels  92.4 us (98%)
    pallas_call x1, Pallas kernels, per_device(): pl.pallas_call(block_kernel, out_shape=(jax.ShapeDtypeStruct((D // 256, M...  86.9 us
    pallas_call x1, Pallas kernels, per_device(): pl.pallas_call(mix_kernel, out_shape=jax.ShapeDtypeStruct((TILES, TILE, D...  5.44 us

profile of v5, /device:TPU:8, one launch (start us, length us, event | category | flops | bytes accessed | tf_op | source)
XLA Modules:
  0.0 92.5 jit_solution(3383676217558160431)
XLA Ops:
  0.0 86.9 %block.1 = (bf16[8,256,256]{2,1,0:T(8,128)(2,1)}, f32[8,256]{1,0:T(8,128)}) custom-call(bf16[1024,2048]{1,0:T(8,128)(2,1)} %tokens.1, bf16[8,8,1024]{2,1,0:T(8,128)(2,1)} %bitcast.10, bf16[64,256]{1,0:T(8,128)(2,1)} %wk.1, bf16[64,256]{1,0:T(8,128)(2,1)} %wv.1, bf16[8,8,1024]{2,1,0:T(8,128)(2,1)} %bitcast.11, s32[1,4096]{1,0:T(1,128)} %bitcast.12, ...), custom_call_target="tpu_custom_call" | custom-call | tf_op jit(solution)/shard_map/block/pallas_call | solution.py:600
  86.9 5.4 %mix.1 = bf16[2,512,2048]{2,1,0:T(8,128)(2,1)} custom-call(bf16[2,512,2048]{2,1,0:T(8,128)(2,1)} %bitcast.9, bf16[8,256,256]{2,1,0:T(8,128)(2,1)} %get-tuple-element.7.block_out, f32[8,256]{1,0:T(8,128)} %get-tuple-element.8.meta), custom_call_target="tpu_custom_call" | custom-call | tf_op jit(solution)/shard_map/mix/pallas_call | solution.py:666
